TPU v7x, 32 devices: a whole 2x2x4 slice. The times are simulated.
32 devices in a mesh: patch: 32 (over z, y, x, core).
Axes of the slice: x: 2, y: 2, z: 4, core: 2. Of those that a mesh axis runs over, the one named last changes fastest.
Arguments:
- atm_flux: bfloat16 [8, 98304], P(None, 'patch'), may hold values from -6 to 6
- remap_send: int32 [32, 5, 8], P('patch'), may hold values from 0 to 23
- remap_target: int32 [32, 5, 8], P('patch'), may hold values from 0 to 31
- remap_counts: int32 [32, 5], P('patch'), may hold values from 0 to 8, as said below
- remap_weights: bfloat16 [32, 5, 8, 128, 128], P('patch'), may hold values from -0.5 to 0.5
- coupling: float32 [2, 8], replicated, may hold values from -2 to 2
- tracer: float32 [2, 128, 131072], P(None, None, 'patch'), may hold values from -6 to 6
- wet: int32 [131072], P('patch'), may hold values from 0 to 1
- mix_inverse: float32 [1024, 128, 128], P('patch')
- halo_send: int32 [32, 4, 2, 128], P('patch'), may hold values from 0 to 4095
- halo_ghost: int32 [32, 4, 2, 128], P('patch'), may hold values from 0 to 4095
- halo_rows: int32 [32, 4], P('patch'), may hold values from 0 to 2, as said below
Outputs:
- ocean_flux: float32 [8, 131072], P(None, 'patch')
- tracer_out: float32 [2, 128, 131072], P(None, None, 'patch')
Inputs may be any that keep to these rules, and one draw needn't show every extreme that they name: `remap_counts`: some entry equals 8. `halo_rows`: some entry equals 2.
All inputs are finite; a program needn't handle non-finite values.
Results may differ from a plain program's by a relative error of at most 0.0003.
Values may be sent and summed in bfloat16 or wider, within the bound.
No kernel may reach another device: no remote copies, remote signals or barrier semaphores. Data moves between devices by JAX's collectives and lax.ppermute only.
A program may use at most 64 MiB of HBM per device.

v0:
```python
import jax
import jax.numpy as jnp
from jax import lax
from jax.sharding import PartitionSpec as P


def shifted(array, axis, by):
    length = lax.axis_size(axis)
    return lax.ppermute(array, axis, [(i, (i + by) % length) for i in range(length)])


def route_fluxes(outgoing, offsets):
    pieces = [shifted(outgoing[index], "patch", offsets[index]) for index in range(len(offsets))]
    return jnp.stack(pieces)


def route_halo(outgoing, offsets):
    pieces = [shifted(outgoing[index], "patch", offsets[index]) for index in range(len(offsets))]
    return jnp.stack(pieces)


def body(
    atm_flux,
    remap_send,
    remap_target,
    remap_counts,
    remap_weights,
    coupling,
    tracer,
    wet,
    mix_inverse,
    halo_send,
    halo_ghost,
    halo_rows,
):
    offset_count = remap_send.shape[1]
    radius = offset_count // 2
    capacity = remap_send.shape[2]
    block_cells = remap_weights.shape[-1]
    flux_count = atm_flux.shape[0]
    tracers, levels, ocean_cells = tracer.shape
    ocean_blocks = ocean_cells // block_cells
    atm_blocks = atm_flux.shape[1] // block_cells
    wetf = wet.astype(jnp.float32)
    blocks = atm_flux.reshape(flux_count, atm_blocks, block_cells)
    chooser = (
        remap_send[0].reshape(-1)[:, None] == jnp.arange(atm_blocks, dtype=jnp.int32)[None, :]
    ).astype(jnp.bfloat16)
    selected = jnp.einsum(
        "sa,fab->sfb", chooser, blocks, preferred_element_type=jnp.float32
    ).astype(jnp.bfloat16)
    outgoing = selected.reshape(offset_count, capacity, flux_count, block_cells)
    flux_offsets = [index - radius for index in range(offset_count)]
    arrived = route_fluxes(outgoing, flux_offsets)
    in_use = (jnp.arange(capacity, dtype=jnp.int32)[None, :] < remap_counts[0][:, None]).astype(
        jnp.float32
    )
    contrib = jnp.einsum(
        "dcfi,dcij->dcfj", arrived, remap_weights[0], preferred_element_type=jnp.float32
    )
    contrib = contrib * in_use[:, :, None, None]
    table = (remap_target[0][..., None] == jnp.arange(ocean_blocks, dtype=jnp.int32)).astype(
        jnp.float32
    )
    ocean_flux = (
        jnp.einsum("dcb,dcfj->fbj", table, contrib, precision=lax.Precision.HIGHEST).reshape(
            flux_count, ocean_cells
        )
        * wetf
    )
    surface = jnp.dot(coupling, ocean_flux, precision=lax.Precision.HIGHEST)
    rhs = jnp.concatenate([tracer[:, 0:1, :] + surface[:, None, :], tracer[:, 1:, :]], axis=1)
    shaped = rhs.reshape(tracers, levels, ocean_blocks, block_cells)
    solved = jnp.einsum(
        "blk,tkbc->tlbc", mix_inverse, shaped, precision=lax.Precision.HIGHEST
    ).reshape(tracers, levels, ocean_cells)
    mixed = wetf * solved + (1.0 - wetf) * tracer
    sent = mixed.astype(jnp.bfloat16)
    halo_count = halo_send.shape[1]
    halo_depth = halo_send.shape[2]
    lanes = halo_send.shape[3]
    picks = halo_count * halo_depth * lanes
    cell_ids = jnp.arange(ocean_cells, dtype=jnp.int32)
    source_table = (cell_ids[:, None] == halo_send[0].reshape(-1)[None, :]).astype(jnp.bfloat16)
    gathered = jnp.dot(
        sent.reshape(tracers * levels, ocean_cells),
        source_table,
        preferred_element_type=jnp.float32,
    ).astype(jnp.bfloat16)
    gathered = gathered.reshape(tracers, levels, halo_count, halo_depth, lanes)
    halo_offsets = [index - radius for index in range(radius)] + [
        index + 1 for index in range(radius)
    ]
    halo_out = jnp.transpose(gathered, (2, 3, 0, 1, 4))
    received = route_halo(halo_out, halo_offsets)
    values = (
        jnp.transpose(received, (2, 3, 0, 1, 4))
        .reshape(tracers * levels, picks)
        .astype(jnp.float32)
    )
    ghost_table = (halo_ghost[0].reshape(-1)[:, None] == cell_ids[None, :]).astype(jnp.float32)
    flat_mixed = mixed.reshape(tracers * levels, ocean_cells)
    current = lax.dot_general(
        flat_mixed, ghost_table, (((1,), (1,)), ((), ())), precision=lax.Precision.HIGHEST
    )
    ghost_wet = jnp.dot(ghost_table, wetf, precision=lax.Precision.HIGHEST)
    rows_used = (jnp.arange(halo_depth, dtype=jnp.int32)[None, :] < halo_rows[0][:, None]).astype(
        jnp.float32
    )
    weight = (
        jnp.broadcast_to(rows_used[:, :, None], (halo_count, halo_depth, lanes)).reshape(-1)
        * ghost_wet
    )
    increment = 0.25 * (values - current) * weight[None, :]
    added = jnp.dot(increment, ghost_table, precision=lax.Precision.HIGHEST)
    tracer_out = (flat_mixed + added).reshape(tracers, levels, ocean_cells)
    return (ocean_flux, tracer_out)


def solution(mesh):
    return jax.shard_map(
        body,
        mesh=mesh,
        in_specs=(
            P(None, "patch"),
            P("patch", None, None),
            P("patch", None, None),
            P("patch", None),
            P("patch", None, None, None, None),
            P(),
            P(None, None, "patch"),
            P("patch"),
            P("patch", None, None),
            P("patch", None, None, None),
            P("patch", None, None, None),
            P("patch", None),
        ),
        out_specs=(P(None, "patch"), P(None, None, "patch")),
        check_vma=False,
    )
```

profile of v0, /device:TPU:1, one launch (start us, length us, event | category | flops | bytes accessed | tf_op | source)
XLA Modules:
  0.0 113.5 jit_solution(16242526582116591750)
XLA Ops:
  0.6 0.0 copy-start
  0.7 0.8 reduce
  1.5 0.1 eq.60
  1.6 1.0 convolution_convert_fusion
  2.6 6.1 %collective-permute-start = (bf16[8,8,128]{2,0,1:T(8,128)(2,1)S(1)}, bf16[8,8,128]{2,0,1:T(8,128)(2,1)S(1)}, u32[]{:S(2)}, u32[]{:S(2)}) collective-permute-start(bf16[8,8,128]{2,0,1:T(8,128)(2,1)S(1)} %get-tuple-element.12), channel_id=1, source_target_pairs={{0,30},{1,31},{2,0},{3,1},{4,2},{5,3},{6,4},{7,5},{8,6},{9,7},{10,... | collective-permute-start | bytes 49160 | tf_op jit(solution)/shard_map/ppermute | solution.py:9
  8.7 1.0 collective-permute-start.1
  9.7 0.0 collective-permute-start.2
  9.7 0.8 collective-permute-start.3
  10.4 0.0 collective-permute-start.4
  10.4 0.7 convert_element_type.41
  11.2 0.7 broadcast_subtract_fusion
  11.9 0.7 fusion.34
  12.6 8.2 %fusion.1 = f32[1,1024]{1,0:T(1,128)S(1)} fusion(f32[4096,1]{0,1:T(1,128)S(1)} %bitcast.96, s32[1024]{0:T(1024)} %bitcast.108), kind=kOutput, calls=%fused_computation.2 | convolution fusion | flops 54525952 | bytes 24576 | tf_op jit(solution)/shard_map/dot_general | solution.py:106
  20.8 0.1 fusion.35
  20.9 1.0 slice.43
  21.9 0.0 copy-start.6
  21.9 5.8 %copy.36 = f32[2,128,4096]{1,2,0:T(8,128)} copy(f32[2,128,4096]{2,1,0:T(8,128)} %param.18) | data formatting | bytes 8388608 | tf_op args[6]
  27.7 0.0 copy-start.7
  27.7 5.4 %slice.54 = f32[2,127,4096]{1,2,0:T(8,128)} slice(f32[2,128,4096]{1,2,0:T(8,128)} %copy.36), slice={[0:2], [1:128], [0:4096]} | slice | bytes 8323072 | tf_op jit(solution)/shard_map/slice | solution.py:72
  33.1 0.0 collective-permute-done.1
  33.2 0.4 fusion.22
  33.6 0.3 convolution_bitcast_fusion.1
  34.0 0.1 bitcast_multiply_fusion.1
  34.1 0.0 copy-start.4
  34.1 0.3 fusion.9
  34.4 2.7 %copy.37 = f32[2,1,4096]{1,2,0:T(8,128)} copy(f32[2,1,4096]{2,0,1:T(2,128)S(1)} %fusion.9) | data formatting | bytes 65536 | tf_op jit(solution)/shard_map/add | solution.py:72
  37.1 4.6 %pad_maximum_fusion = f32[2,128,4096]{1,2,0:T(8,128)S(1)} fusion(f32[2,127,4096]{1,2,0:T(8,128)} %slice.54, f32[2,1,4096]{1,2,0:T(8,128)} %copy.37), kind=kLoop, calls=%fused_computation.13 | loop fusion | flops 1048576 | bytes 8388608 | tf_op jit(solution)/shard_map/concatenate | solution.py:72
  41.7 4.5 %fusion.13 = f32[2,128,32,128]{1,3,0,2:T(8,128)S(1)} fusion(f32[2,128,32,128]{1,3,2,0:T(8,128)S(1)} %bitcast.91, f32[32,128,128]{2,1,0:T(8,128)S(1)} %copy-done), kind=kOutput, calls=%fused_computation.18 | convolution fusion | flops 1610612736 | bytes 10485760 | tf_op jit(solution)/shard_map/blk,tkbc->tlbc/dot_general | solution.py:74
  46.2 0.0 copy-start.1
  46.2 0.3 copy.39
  46.5 1.9 %copy-done.1 = f32[2,128,4096]{1,2,0:T(8,128)S(1)} copy-done((f32[2,128,4096]{1,2,0:T(8,128)S(1)}, f32[2,128,4096]{1,2,0:T(8,128)}, u32[]{:S(2)}) %copy-start.1) | copy-done | bytes 4194328
  48.4 4.1 %fusion.36 = (bf16[2,128,4096]{1,2,0:T(8,128)(2,1)}, f32[2,128,4096]{1,2,0:T(8,128)}) fusion(f32[2,128,4096]{1,2,0:T(8,128)S(1)} %copy-done.1, f32[4096]{0:T(1024)S(1)} %broadcast_subtract_fusion, f32[2,128,32,128]{1,3,2,0:T(8,128)S(1)} %copy.39, f32[4096]{0:T(1024)S(1)} %convert_element_type.41), kind=kLoop, calls=%fused_computation.56 | loop fusion | flops 4194304 | bytes 14712832 | tf_op jit(solution)/shard_map/convert_element_type | solution.py:78
  52.5 4.2 %copy.42 = bf16[2,128,4096]{2,1,0:T(8,128)(2,1)} copy(bf16[2,128,4096]{1,2,0:T(8,128)(2,1)} %get-tuple-element.2) | data formatting | bytes 4194304 | tf_op jit(solution)/shard_map/convert_element_type | solution.py:78
  56.6 4.9 %fusion.21 = bf16[256,1024]{1,0:T(8,128)(2,1)S(1)} fusion(bf16[256,4096]{1,0:T(8,128)(2,1)} %bitcast.94, s32[1024]{0:T(1024)S(1)} %bitcast.107), kind=kOutput, calls=%fused_computation.24 | convolution fusion | flops 2151940096 | bytes 2625536 | tf_op jit(solution)/shard_map/dot_general | solution.py:85
  61.5 0.4 reshape.109
  61.9 0.4 copy.66
  62.3 0.4 slice_bitcast_fusion.3
  62.7 5.1 %collective-permute-start.5 = (bf16[2,2,128,128]{3,0,2,1:T(2,128)(2,1)S(1)}, bf16[2,2,128,128]{3,0,2,1:T(2,128)(2,1)S(1)}, u32[]{:S(2)}, u32[]{:S(2)}) collective-permute-start(bf16[2,2,128,128]{3,0,2,1:T(2,128)(2,1)S(1)} %get-tuple-element.4), channel_id=1, source_target_pairs={{0,30},{1,31},{2,0},{3,1},{4,2},{5,3},{6,4},{7,5},{8,6},{9,7},{10,... | collective-permute-start | bytes 393224 | tf_op jit(solution)/shard_map/ppermute | solution.py:9
  67.8 0.3 collective-permute-start.6
  68.1 1.4 %collective-permute-start.7 = (bf16[2,2,128,128]{3,0,2,1:T(2,128)(2,1)S(1)}, bf16[2,2,128,128]{3,0,2,1:T(2,128)(2,1)S(1)}, u32[]{:S(2)}, u32[]{:S(2)}) collective-permute-start(bf16[2,2,128,128]{3,0,2,1:T(2,128)(2,1)S(1)} %get-tuple-element.6), channel_id=1, source_target_pairs={{0,1},{1,2},{2,3},{3,4},{4,5},{5,6},{6,7},{7,8},{8,9},{9,10},{10,1... | collective-permute-start | bytes 393224 | tf_op jit(solution)/shard_map/ppermute | solution.py:9
  69.5 0.1 broadcast_in_dim.5
  69.6 5.6 %copy.41 = f32[2,128,4096]{2,1,0:T(8,128)} copy(f32[2,128,4096]{1,2,0:T(8,128)} %get-tuple-element.3) | data formatting | bytes 8388608 | tf_op jit(solution)/shard_map/add | solution.py:77
  75.2 3.6 %collective-permute-done.8 = bf16[2,2,128,128]{3,0,2,1:T(2,128)(2,1)S(1)} collective-permute-done((bf16[2,2,128,128]{3,0,2,1:T(2,128)(2,1)S(1)}, bf16[2,2,128,128]{3,0,2,1:T(2,128)(2,1)S(1)}, u32[]{:S(2)}, u32[]{:S(2)}) %collective-permute-start.8) | collective-permute-done | bytes 131104 | tf_op jit(solution)/shard_map/ppermute | solution.py:9
  78.8 0.7 copy-done.5
  79.5 1.6 %convert_bitcast_fusion = f32[2,128,4,2,128]{4,3,2,1,0:T(2,128)S(1)} fusion(bf16[1,2,2,128,128]{4,1,0,3,2:T(2,128)(2,1)} %bitcast.100, bf16[1,2,2,128,128]{4,1,0,3,2:T(2,128)(2,1)S(1)} %bitcast.99, bf16[1,2,2,128,128]{4,1,0,3,2:T(2,128)(2,1)S(1)} %bitcast.98, bf16[1,2,2,128,128]{4,1,0,3,2:T(2,128)(2,1)S(1)} %bitcast.97), kind=kLoop, calls=%fused_computation.28 | loop fusion | flops 1048576 | bytes 1572864 | tf_op jit(solution)/shard_map/convert_element_type | solution.py:99
  81.1 1.8 %reshape.112 = f32[256,1024]{1,0:T(8,128)} reshape(f32[2,128,4,2,128]{4,3,2,1,0:T(2,128)S(1)} %convert_bitcast_fusion) | data formatting | bytes 2097152 | tf_op jit(solution)/shard_map/convert_element_type | solution.py:99
  82.9 20.4 %fusion.20 = f32[256,1024]{1,0:T(8,128)S(1)} fusion(f32[256,1024]{1,0:T(8,128)} %reshape.112, f32[256,4096]{1,0:T(8,128)} %bitcast.92, s32[1024]{0:T(1024)S(1)} %bitcast.109, f32[1024]{0:T(1024)S(1)} %multiply_multiply_fusion), kind=kOutput, calls=%fused_computation.23 | convolution fusion | flops 12889620480 | bytes 6299648 | tf_op jit(solution)/shard_map/dot_general | solution.py:103
  103.4 10.1 %fusion.8 = f32[256,4096]{1,0:T(8,128)} fusion(f32[256,4096]{1,0:T(8,128)S(1)} %bitcast.93, f32[256,1024]{1,0:T(8,128)S(1)} %fusion.20, s32[1024]{0:T(1024)S(1)} %bitcast.110), kind=kOutput, calls=%fused_computation.10 | convolution fusion | flops 12890144768 | bytes 9441280 | tf_op jit(solution)/shard_map/dot_general | solution.py:115
  (31 shorter events, 0.1 us)
Async XLA Ops:
  0.6 41.1 %copy-start = (f32[32,128,128]{2,1,0:T(8,128)S(1)}, f32[32,128,128]{2,1,0:T(8,128)}, u32[]{:S(2)}) copy-start(f32[32,128,128]{2,1,0:T(8,128)} %param.20) | copy-start | bytes 6291460
  0.6 20.2 %copy-start.8 = (s32[1,4]{1,0:T(1,128)S(1)}, s32[1,4]{1,0:T(1,128)}, u32[]{:S(2)}) copy-start(s32[1,4]{1,0:T(1,128)} %param.23) | copy-start | bytes 52
  2.6 30.5 %collective-permute-start = (bf16[8,8,128]{2,0,1:T(8,128)(2,1)S(1)}, bf16[8,8,128]{2,0,1:T(8,128)(2,1)S(1)}, u32[]{:S(2)}, u32[]{:S(2)}) collective-permute-start(bf16[8,8,128]{2,0,1:T(8,128)(2,1)S(1)} %get-tuple-element.12), channel_id=1, source_target_pairs={{0,30},{1,31},{2,0},{3,1},{4,2},{5,3},{6,4},{7,5},{8,6},{9,7},{10,... | collective-permute-start | bytes 49160 | tf_op jit(solution)/shard_map/ppermute | solution.py:9
  8.7 24.4 %collective-permute-start.1 = (bf16[8,8,128]{2,0,1:T(8,128)(2,1)S(1)}, bf16[8,8,128]{2,0,1:T(8,128)(2,1)S(1)}, u32[]{:S(2)}, u32[]{:S(2)}) collective-permute-start(bf16[8,8,128]{2,0,1:T(8,128)(2,1)S(1)} %get-tuple-element.11), channel_id=1, source_target_pairs={{0,31},{1,0},{2,1},{3,2},{4,3},{5,4},{6,5},{7,6},{8,7},{9,8},{10,9... | collective-permute-start | bytes 49160 | tf_op jit(solution)/shard_map/ppermute | solution.py:9
  9.7 23.5 %collective-permute-start.2 = (bf16[8,8,128]{2,0,1:T(8,128)(2,1)S(1)}, bf16[8,8,128]{2,0,1:T(8,128)(2,1)S(1)}, u32[]{:S(2)}, u32[]{:S(2)}) collective-permute-start(bf16[8,8,128]{2,0,1:T(8,128)(2,1)S(1)} %get-tuple-element.10), channel_id=1, source_target_pairs={{0,0},{1,1},{2,2},{3,3},{4,4},{5,5},{6,6},{7,7},{8,8},{9,9},{10,10... | collective-permute-start | bytes 49160 | tf_op jit(solution)/shard_map/ppermute | solution.py:9
  9.7 23.5 %collective-permute-start.3 = (bf16[8,8,128]{2,0,1:T(8,128)(2,1)S(1)}, bf16[8,8,128]{2,0,1:T(8,128)(2,1)S(1)}, u32[]{:S(2)}, u32[]{:S(2)}) collective-permute-start(bf16[8,8,128]{2,0,1:T(8,128)(2,1)S(1)} %get-tuple-element.9), channel_id=1, source_target_pairs={{0,1},{1,2},{2,3},{3,4},{4,5},{5,6},{6,7},{7,8},{8,9},{9,10},{10,1... | collective-permute-start | bytes 49160 | tf_op jit(solution)/shard_map/ppermute | solution.py:9
  10.4 22.7 %collective-permute-start.4 = (bf16[8,8,128]{2,0,1:T(8,128)(2,1)S(1)}, bf16[8,8,128]{2,0,1:T(8,128)(2,1)S(1)}, u32[]{:S(2)}, u32[]{:S(2)}) collective-permute-start(bf16[8,8,128]{2,0,1:T(8,128)(2,1)S(1)} %get-tuple-element.8), channel_id=1, source_target_pairs={{0,2},{1,3},{2,4},{3,5},{4,6},{5,7},{6,8},{7,9},{8,10},{9,11},{10,... | collective-permute-start | bytes 49160 | tf_op jit(solution)/shard_map/ppermute | solution.py:9
  21.9 5.8 %copy-start.6 = (s32[1,5,8]{2,0,1:T(1,128)S(1)}, s32[1,5,8]{2,0,1:T(1,128)}, u32[]{:S(2)}) copy-start(s32[1,5,8]{2,0,1:T(1,128)} %param.14) | copy-start | bytes 484
  27.7 5.5 %copy-start.3 = (bf16[1,5,8,128,128]{4,3,2,1,0:T(8,128)(2,1)S(1)}, bf16[1,5,8,128,128]{4,3,2,1,0:T(8,128)(2,1)}, u32[]{:S(2)}) copy-start(bf16[1,5,8,128,128]{4,3,2,1,0:T(8,128)(2,1)} %param.16) | copy-start | bytes 3932164
  27.7 6.4 %copy-start.7 = (f32[2,8]{1,0:T(2,128)S(1)}, f32[2,8]{1,0:T(2,128)}, u32[]{:S(2)}) copy-start(f32[2,8]{1,0:T(2,128)} %param.17) | copy-start | bytes 196
  34.1 7.6 %copy-start.4 = (f32[8,4096]{1,0:T(8,128)}, f32[8,4096]{1,0:T(8,128)S(1)}, u32[]{:S(2)}) copy-start(f32[8,4096]{1,0:T(8,128)S(1)} %bitcast_multiply_fusion.1) | copy-start | bytes 393220
  46.2 2.2 %copy-start.1 = (f32[2,128,4096]{1,2,0:T(8,128)S(1)}, f32[2,128,4096]{1,2,0:T(8,128)}, u32[]{:S(2)}) copy-start(f32[2,128,4096]{1,2,0:T(8,128)} %copy.36) | copy-start | bytes 12582916
  52.5 4.2 %copy-start.9 = (s32[1,4,2,128]{3,2,1,0:T(2,128)S(1)}, s32[1,4,2,128]{3,2,1,0:T(2,128)}, u32[]{:S(2)}) copy-start(s32[1,4,2,128]{3,2,1,0:T(2,128)} %param.21) | copy-start | bytes 12292
  62.7 12.6 %collective-permute-start.5 = (bf16[2,2,128,128]{3,0,2,1:T(2,128)(2,1)S(1)}, bf16[2,2,128,128]{3,0,2,1:T(2,128)(2,1)S(1)}, u32[]{:S(2)}, u32[]{:S(2)}) collective-permute-start(bf16[2,2,128,128]{3,0,2,1:T(2,128)(2,1)S(1)} %get-tuple-element.4), channel_id=1, source_target_pairs={{0,30},{1,31},{2,0},{3,1},{4,2},{5,3},{6,4},{7,5},{8,6},{9,7},{10,... | collective-permute-start | bytes 393224 | tf_op jit(solution)/shard_map/ppermute | solution.py:9
  67.8 7.5 %collective-permute-start.6 = (bf16[2,2,128,128]{3,0,2,1:T(2,128)(2,1)S(1)}, bf16[2,2,128,128]{3,0,2,1:T(2,128)(2,1)S(1)}, u32[]{:S(2)}, u32[]{:S(2)}) collective-permute-start(bf16[2,2,128,128]{3,0,2,1:T(2,128)(2,1)S(1)} %get-tuple-element.7), channel_id=1, source_target_pairs={{0,31},{1,0},{2,1},{3,2},{4,3},{5,4},{6,5},{7,6},{8,7},{9,8},{10,9... | collective-permute-start | bytes 393224 | tf_op jit(solution)/shard_map/ppermute | solution.py:9
  68.1 7.2 %collective-permute-start.7 = (bf16[2,2,128,128]{3,0,2,1:T(2,128)(2,1)S(1)}, bf16[2,2,128,128]{3,0,2,1:T(2,128)(2,1)S(1)}, u32[]{:S(2)}, u32[]{:S(2)}) collective-permute-start(bf16[2,2,128,128]{3,0,2,1:T(2,128)(2,1)S(1)} %get-tuple-element.6), channel_id=1, source_target_pairs={{0,1},{1,2},{2,3},{3,4},{4,5},{5,6},{6,7},{7,8},{8,9},{9,10},{10,1... | collective-permute-start | bytes 393224 | tf_op jit(solution)/shard_map/ppermute | solution.py:9
  69.5 9.3 %collective-permute-start.8 = (bf16[2,2,128,128]{3,0,2,1:T(2,128)(2,1)S(1)}, bf16[2,2,128,128]{3,0,2,1:T(2,128)(2,1)S(1)}, u32[]{:S(2)}, u32[]{:S(2)}) collective-permute-start(bf16[2,2,128,128]{3,0,2,1:T(2,128)(2,1)S(1)} %get-tuple-element.5), channel_id=1, source_target_pairs={{0,2},{1,3},{2,4},{3,5},{4,6},{5,7},{6,8},{7,9},{8,10},{9,11},{10,... | collective-permute-start | bytes 393224 | tf_op jit(solution)/shard_map/ppermute | solution.py:9
  69.6 13.3 %copy-start.10 = (s32[1,4,2,128]{3,2,1,0:T(2,128)S(1)}, s32[1,4,2,128]{3,2,1,0:T(2,128)}, u32[]{:S(2)}) copy-start(s32[1,4,2,128]{3,2,1,0:T(2,128)} %param.22) | copy-start | bytes 12292
  78.8 0.7 copy-start.5
  82.9 20.4 %copy-start.2 = (f32[2,128,4096]{2,1,0:T(8,128)S(1)}, f32[2,128,4096]{2,1,0:T(8,128)}, u32[]{:S(2)}) copy-start(f32[2,128,4096]{2,1,0:T(8,128)} %copy.41) | copy-start | bytes 12582916
where the time goes:
time: 114 us; the launch traced here: 113 us
  matrix products  50.2 us (44%)
  local copies, waits for them, and re-layouts  30.6 us (27%)
  starting transfers between devices  14.7 us (13%)
  other arithmetic  13.5 us (12%)
  waiting for transfers between devices  3.61 us (3%)
    dot_general x1, matrix products, body(): lax.dot_general(flat_mixed, ghost_table, (((1,), (1,)), ((), ())), precis...  20.4 us
    ppermute x9, starting transfers between devices, shifted(): lax.ppermute(array, axis, [(i, (i + by) % length) for i in range(length)])  14.7 us
    dot_general x1, matrix products, body(): added = jnp.dot(increment, ghost_table, precision=lax.Precision.HIGHEST)  10.1 us
    unnamed x28, local copies, waits for them, and re-layouts  8.42 us
    dot_general x1, matrix products, body(): ghost_wet = jnp.dot(ghost_table, wetf, precision=lax.Precision.HIGHEST)  8.22 us
    add x1, local copies, waits for them, and re-layouts, body(): mixed = wetf * solved + (1.0 - wetf) * tracer  5.65 us
    slice x1, local copies, waits for them, and re-layouts, body(): tracer[:, 1:, :]  5.38 us
    dot_general x1, matrix products, body(): jnp.dot(sent.reshape(tracers * levels, ocean_cells), source_table, prefer...  4.92 us
  transfers between devices with their start and end apart: 9, of which 1 were waited for; matrix products, arithmetic and copies ran while one was open for 25% of the time, Pallas kernels for 0%

commit v1 on v0

v1 whole, which is shorter than its diff:
```python
import functools

import jax
import jax.numpy as jnp
from jax import lax
from jax.experimental import pallas as pl
from jax.experimental.pallas import tpu as pltpu
from jax.sharding import PartitionSpec as P

F32 = jnp.float32
BF16 = jnp.bfloat16


def shifted(array, axis, by):
    length = lax.axis_size(axis)
    return lax.ppermute(array, axis, [(i, (i + by) % length) for i in range(length)])


def select_kernel(send_ref, atm_ref, *out_refs):
    offsets, capacity = send_ref.shape[1], send_ref.shape[2]
    cells = out_refs[0].shape[-1]
    for d in range(offsets):
        for c in range(capacity):
            start = pl.multiple_of(send_ref[0, d, c] * cells, cells)
            out_refs[d][c] = atm_ref[:, pl.ds(start, cells)]


def select_blocks(remap_send, atm_flux, cells):
    offsets, capacity = remap_send.shape[1], remap_send.shape[2]
    fluxes = atm_flux.shape[0]
    return pl.pallas_call(
        select_kernel,
        out_shape=[jax.ShapeDtypeStruct((capacity, fluxes, cells), BF16)] * offsets,
        in_specs=[
            pl.BlockSpec(memory_space=pltpu.SMEM),
            pl.BlockSpec(memory_space=pltpu.VMEM),
        ],
        out_specs=[pl.BlockSpec(memory_space=pltpu.VMEM)] * offsets,
        name="select_blocks",
    )(remap_send, atm_flux)


def split(x):
    high = x.astype(BF16)
    low = (x - high.astype(F32)).astype(BF16)
    return high, low


def lane_onehot(index_rows, cells):
    parts = []
    for q in range(index_rows.shape[0]):
        lane = index_rows[q : q + 1, :] & (cells - 1)
        sub = lax.broadcasted_iota(jnp.int32, (cells, index_rows.shape[1]), 0)
        parts.append(jnp.where(sub == lane, 1.0, 0.0).astype(BF16))
    return jnp.concatenate(parts, axis=1)


def mix_kernel(
    target_ref, count_ref, coupling_ref, *rest, offsets, capacity, group
):
    pieces = rest[:offsets]
    (wet_ref, send_ref, weights_hbm, tracer_hbm, inverse_hbm) = rest[offsets : offsets + 5]
    outs = rest[offsets + 5 :]
    flux_out = outs[0]
    mixed_hbm = outs[1]
    halo_count = offsets - 1
    halo_outs = outs[2 : 2 + halo_count]
    (
        weights, tracer, inverse, mixed, sent, acc, onehot, base,
        weight_sem, in_sems, out_sems,
    ) = outs[2 + halo_count :]
    tracers, levels, ocean_cells = tracer.shape
    cells = weights.shape[-1]
    blocks = ocean_cells // cells
    groups = blocks // group
    span = group * cells
    fluxes = flux_out.shape[0]

    def load(g):
        lanes = pl.ds(g * span, span)
        return (
            pltpu.make_async_copy(
                tracer_hbm.at[:, :, lanes], tracer.at[:, :, lanes], in_sems.at[0, g]
            ),
            pltpu.make_async_copy(
                inverse_hbm.at[pl.ds(g * group, group)],
                inverse.at[pl.ds(g * group, group)],
                in_sems.at[1, g],
            ),
        )

    def store(g):
        lanes = pl.ds(g * span, span)
        return pltpu.make_async_copy(
            mixed.at[:, :, lanes], mixed_hbm.at[:, :, lanes], out_sems.at[g]
        )

    weight_copy = pltpu.make_async_copy(weights_hbm, weights, weight_sem)
    weight_copy.start()
    for g in range(groups):
        for copy in load(g):
            copy.start()

    base[...] = lane_onehot(send_ref[...], cells)
    block_row = jnp.concatenate(
        [send_ref[q : q + 1, :] // cells for q in range(send_ref.shape[0])], axis=1
    )

    acc[...] = jnp.zeros_like(acc)
    weight_copy.wait()
    for d in range(offsets):
        for c in range(capacity):
            contrib = jnp.dot(
                pieces[d][c], weights[d * capacity + c], preferred_element_type=F32
            )
            used = jnp.where(c < count_ref[0, d], 1.0, 0.0).astype(F32)
            start = pl.multiple_of(target_ref[0, d, c] * cells, cells)
            acc[:, pl.ds(start, cells)] += contrib * used

    sub = lax.broadcasted_iota(jnp.int32, (fluxes, cells), 0)
    couple = []
    for t in range(tracers):
        col = jnp.zeros((fluxes, cells), F32)
        for f in range(fluxes):
            col = jnp.where(sub == f, coupling_ref[t, f], col)
        couple.append(col)
    top = lax.broadcasted_iota(jnp.int32, (levels, cells), 0) == 0

    for g in range(groups):
        for copy in load(g):
            copy.wait()
        for i in range(group):
            b = g * group + i
            lanes = slice(b * cells, (b + 1) * cells)
            wet = wet_ref[b : b + 1, :].astype(F32)
            flux = acc[:, lanes] * wet
            flux_out[:, lanes] = flux
            highs, lows, raw = [], [], []
            for t in range(tracers):
                surface = jnp.sum(couple[t] * flux, axis=0, keepdims=True)
                value = tracer[t, :, lanes]
                raw.append(value)
                high, low = split(value + jnp.where(top, surface, 0.0))
                highs.append(high)
                lows.append(low)
            high = jnp.concatenate(highs, axis=1)
            low = jnp.concatenate(lows, axis=1)
            m_high, m_low = split(inverse[b])
            left = jnp.concatenate([m_high, m_low], axis=1)
            right = jnp.concatenate([high, high], axis=0)
            solved = jnp.dot(left, right, preferred_element_type=F32) + jnp.dot(
                m_high, low, preferred_element_type=F32
            )
            for t in range(tracers):
                value = jnp.where(
                    wet > 0.5, solved[:, t * cells : (t + 1) * cells], raw[t]
                )
                mixed[t, :, lanes] = value
                sent[t * levels : (t + 1) * levels, lanes] = value.astype(BF16)
            onehot[lanes, :] = base[...] * jnp.where(block_row == b, 1.0, 0.0).astype(BF16)
        store(g).start()

    picks = onehot.shape[1] // halo_count
    for h in range(halo_count):
        halo_outs[h][...] = jnp.dot(
            sent[...], onehot[:, h * picks : (h + 1) * picks], preferred_element_type=F32
        ).astype(BF16)
    for g in range(groups):
        store(g).wait()


def mix(pieces, remap_target, remap_counts, remap_weights, coupling, tracer, wet, mix_inverse, halo_send):
    offsets, capacity = remap_target.shape[1:]
    tracers, levels, ocean_cells = tracer.shape
    cells = remap_weights.shape[-1]
    blocks = ocean_cells // cells
    fluxes = pieces[0].shape[1]
    halo_count, depth, lanes = halo_send.shape[1:]
    picks = depth * lanes
    group = 4 if blocks % 4 == 0 else 1
    groups = blocks // group
    smem = pl.BlockSpec(memory_space=pltpu.SMEM)
    vmem = pl.BlockSpec(memory_space=pltpu.VMEM)
    hbm = pl.BlockSpec(memory_space=pl.ANY)
    return pl.pallas_call(
        functools.partial(mix_kernel, offsets=offsets, capacity=capacity, group=group),
        out_shape=[
            jax.ShapeDtypeStruct((fluxes, ocean_cells), F32),
            jax.ShapeDtypeStruct(tracer.shape, F32),
        ]
        + [jax.ShapeDtypeStruct((tracers * levels, picks), BF16)] * halo_count,
        in_specs=[smem, smem, smem] + [vmem] * offsets + [vmem, vmem, hbm, hbm, hbm],
        out_specs=[vmem, hbm] + [vmem] * halo_count,
        scratch_shapes=[
            pltpu.VMEM((offsets * capacity, cells, cells), BF16),
            pltpu.VMEM(tracer.shape, F32),
            pltpu.VMEM((blocks, levels, levels), F32),
            pltpu.VMEM(tracer.shape, F32),
            pltpu.VMEM((tracers * levels, ocean_cells), BF16),
            pltpu.VMEM((fluxes, ocean_cells), F32),
            pltpu.VMEM((ocean_cells, halo_count * picks), BF16),
            pltpu.VMEM((cells, halo_count * picks), BF16),
            pltpu.SemaphoreType.DMA,
            pltpu.SemaphoreType.DMA((2, groups)),
            pltpu.SemaphoreType.DMA((groups,)),
        ],
        name="mix",
    )(
        remap_target,
        remap_counts,
        coupling,
        *pieces,
        wet.reshape(blocks, cells),
        halo_send.reshape(halo_count * depth, lanes),
        remap_weights.reshape(offsets * capacity, cells, cells),
        tracer,
        mix_inverse,
    )


def apply_kernel(rows_ref, ghost_ref, wet_ref, *rest, halo_count, depth):
    values = rest[:halo_count]
    mixed_ref, out_ref, base, left = rest[halo_count:]
    tracers, levels, span = mixed_ref.shape
    cells = wet_ref.shape[1]
    group = span // cells
    step = pl.program_id(0)
    rows = tracers * levels
    picks = values[0].shape[1]

    @pl.when(step == 0)
    def _():
        base[...] = lane_onehot(ghost_ref[...], cells)
        for h in range(halo_count):
            left[0:rows, h * picks : (h + 1) * picks] = values[h][...]
        left[rows:, :] = jnp.ones((left.shape[0] - rows, left.shape[1]), BF16)

    block_row = []
    for h in range(halo_count):
        for r in range(depth):
            q = h * depth + r
            block = ghost_ref[q : q + 1, :] // cells
            block_row.append(jnp.where(r < rows_ref[0, h], block, -1))
    block_row = jnp.concatenate(block_row, axis=1)
    onehots = []
    for i in range(group):
        b = step * group + i
        onehots.append(base[...] * jnp.where(block_row == b, 1.0, 0.0).astype(BF16))
    onehot = jnp.concatenate(onehots, axis=0)
    total = lax.dot_general(
        left[...], onehot, (((1,), (1,)), ((), ())), preferred_element_type=F32
    )
    count = total[rows : rows + 1, :]
    for i in range(group):
        b = step * group + i
        lanes = slice(i * cells, (i + 1) * cells)
        quarter = 0.25 * wet_ref[pl.ds(b, 1), :].astype(F32)
        keep = 1.0 - quarter * count[:, lanes]
        for t in range(tracers):
            out_ref[t, :, lanes] = (
                mixed_ref[t, :, lanes] * keep
                + total[t * levels : (t + 1) * levels, lanes] * quarter
            )


def apply_halo(values, mixed, wet, halo_ghost, halo_rows):
    tracers, levels, ocean_cells = mixed.shape
    halo_count, depth, lanes = halo_ghost.shape[1:]
    cells = lanes
    blocks = ocean_cells // cells
    picks = halo_count * depth * lanes
    group = 4 if blocks % 4 == 0 else 1
    span = group * cells
    smem = pl.BlockSpec(memory_space=pltpu.SMEM)
    vmem = pl.BlockSpec(memory_space=pltpu.VMEM)
    block = pl.BlockSpec((tracers, levels, span), lambda g: (0, 0, g))
    return pl.pallas_call(
        functools.partial(apply_kernel, halo_count=halo_count, depth=depth),
        grid=(blocks // group,),
        out_shape=jax.ShapeDtypeStruct(mixed.shape, F32),
        in_specs=[smem, vmem, vmem] + [vmem] * halo_count + [block],
        out_specs=block,
        scratch_shapes=[
            pltpu.VMEM((cells, picks), BF16),
            pltpu.VMEM((tracers * levels + 16, picks), BF16),
        ],
        name="apply_halo",
    )(
        halo_rows,
        halo_ghost.reshape(halo_count * depth, lanes),
        wet.reshape(blocks, cells),
        *values,
        mixed,
    )


def body(
    atm_flux,
    remap_send,
    remap_target,
    remap_counts,
    remap_weights,
    coupling,
    tracer,
    wet,
    mix_inverse,
    halo_send,
    halo_ghost,
    halo_rows,
):
    offsets = remap_send.shape[1]
    radius = offsets // 2
    cells = remap_weights.shape[-1]
    outgoing = select_blocks(remap_send, atm_flux, cells)
    pieces = [
        outgoing[d] if d == radius else shifted(outgoing[d], "patch", d - radius)
        for d in range(offsets)
    ]
    ocean_flux, mixed, *halo_out = mix(
        pieces, remap_target, remap_counts, remap_weights[0], coupling, tracer, wet,
        mix_inverse, halo_send,
    )
    halo_offsets = [e for e in range(-radius, radius + 1) if e]
    values = [shifted(halo_out[h], "patch", halo_offsets[h]) for h in range(len(halo_out))]
    return ocean_flux, apply_halo(values, mixed, wet, halo_ghost, halo_rows)


def solution(mesh):
    return jax.shard_map(
        body,
        mesh=mesh,
        in_specs=(
            P(None, "patch"),
            P("patch", None, None),
            P("patch", None, None),
            P("patch", None),
            P("patch", None, None, None, None),
            P(),
            P(None, None, "patch"),
            P("patch"),
            P("patch", None, None),
            P("patch", None, None, None),
            P("patch", None, None, None),
            P("patch", None),
        ),
        out_specs=(P(None, "patch"), P(None, None, "patch")),
        check_vma=False,
    )
```

time: 114 us -> 50.6 us (0.44)
  matrix products: 50.2 us -> 0 us
  local copies, waits for them, and re-layouts: 30.6 us -> 3.8 us
  Pallas kernels: 0 us -> 21.1 us
  other arithmetic: 13.5 us -> 0 us
  waiting for transfers between devices: 3.61 us -> 12.3 us
  starting transfers between devices: 14.7 us -> 11.9 us
    dot_general x9 -> x0, matrix products: 50.2 us -> none  [the longest x1 20.4 us: body(): lax.dot_general(flat_mixed, ghost_table, (((1,), (1,)), ((), ())), precis...]
    pallas_call x0 -> x3, Pallas kernels: none -> 21.1 us  [the longest x1 10.5 us: mix(): pl.pallas_call(functools.partial(mix_kernel, offsets=offsets, capacity=ca...]
    ppermute x9 -> x8, waiting for transfers between devices: 3.61 us -> 12.3 us  [shifted(): lax.ppermute(array, axis, [(i, (i + by) % length) for i in range(length)])]
    add x2 -> x0, local copies, waits for them, and re-layouts: 8.35 us -> none  [the longest x1 5.65 us: body(): mixed = wetf * solved + (1.0 - wetf) * tracer]
    convert_element_type x5 -> x0, other arithmetic: 7.23 us -> none  [the longest x1 4.1 us: body(): sent = mixed.astype(jnp.bfloat16)]
    slice x3 -> x0, local copies, waits for them, and re-layouts: 6.38 us -> none  [the longest x1 5.38 us: body(): tracer[:, 1:, :]]
    convert_element_type x2 -> x0, local copies, waits for them, and re-layouts: 5.96 us -> none  [the longest x1 4.15 us: body(): sent = mixed.astype(jnp.bfloat16)]
    unnamed x28 -> x18, local copies, waits for them, and re-layouts: 8.42 us -> 3.8 us
  transfers between devices with their start and end apart: 9 -> 8, of which waited for: 1 -> 5; matrix products, arithmetic and copies ran while one was open for 25% -> 3% of each run, Pallas kernels for 0% -> 0%
where the time goes in v1:
time: 50.6 us; the launch traced here: 49.9 us
  Pallas kernels  21.1 us (42%)
  waiting for transfers between devices  12.3 us (24%)
  starting transfers between devices  11.9 us (24%)
  local copies, waits for them, and re-layouts  3.8 us (8%)
  between operations  0.66 us (1%)
    ppermute x8, waiting for transfers between devices, shifted(): lax.ppermute(array, axis, [(i, (i + by) % length) for i in range(length)])  12.3 us
    ppermute x8, starting transfers between devices, shifted(): lax.ppermute(array, axis, [(i, (i + by) % length) for i in range(length)])  11.9 us
    pallas_call x1, Pallas kernels, mix(): pl.pallas_call(functools.partial(mix_kernel, offsets=offsets, capacity=ca...  10.5 us
    pallas_call x1, Pallas kernels, apply_halo(): pl.pallas_call(functools.partial(apply_kernel, halo_count=halo_count, dep...  9.12 us
    unnamed x18, local copies, waits for them, and re-layouts  3.8 us
    pallas_call x1, Pallas kernels, select_blocks(): pl.pallas_call(select_kernel, out_shape=[jax.ShapeDtypeStruct((capacity,...  1.49 us
  transfers between devices with their start and end apart: 8, of which 5 were waited for; matrix products, arithmetic and copies ran while one was open for 3% of the time, Pallas kernels for 0%

profile of v1, /device:TPU:1, one launch (start us, length us, event | category | flops | bytes accessed | tf_op | source)
XLA Modules:
  0.0 49.9 jit_solution(7713670128433816954)
XLA Ops:
  0.6 1.3 %copy.14.send_ref = s32[1,5,8]{2,1,0:T(8,128)} copy(s32[1,5,8]{2,0,1:T(1,128)} %param.13) | data formatting | bytes 320 | tf_op args[1]
  1.9 1.5 %select_blocks.1 = (bf16[8,8,128]{2,1,0:T(8,128)(2,1)}, bf16[8,8,128]{2,1,0:T(8,128)(2,1)}, bf16[8,8,128]{2,1,0:T(8,128)(2,1)}, bf16[8,8,128]{2,1,0:T(8,128)(2,1)}, bf16[8,8,128]{2,1,0:T(8,128)(2,1)}) custom-call(s32[1,5,8]{2,1,0:T(8,128)} %copy.14.send_ref, bf16[8,3072]{1,0:T(8,128)(2,1)} %atm_ref.1), custom_call_target="tpu_custom_call" | custom-call | tf_op jit(solution)/shard_map/select_blocks/pallas_call | solution.py:31
  3.4 6.0 %collective-permute-start = (bf16[8,8,128]{2,1,0:T(8,128)(2,1)}, bf16[8,8,128]{2,1,0:T(8,128)(2,1)S(1)}, u32[]{:S(2)}, u32[]{:S(2)}) collective-permute-start(bf16[8,8,128]{2,1,0:T(8,128)(2,1)} %get-tuple-element.13), channel_id=1, source_target_pairs={{0,30},{1,31},{2,0},{3,1},{4,2},{5,3},{6,4},{7,5},{8,6},{9,7},{10,... | collective-permute-start | bytes 49160 | tf_op jit(solution)/shard_map/ppermute | solution.py:16
  9.4 1.0 %collective-permute-start.1 = (bf16[8,8,128]{2,1,0:T(8,128)(2,1)}, bf16[8,8,128]{2,1,0:T(8,128)(2,1)S(1)}, u32[]{:S(2)}, u32[]{:S(2)}) collective-permute-start(bf16[8,8,128]{2,1,0:T(8,128)(2,1)} %get-tuple-element.14), channel_id=1, source_target_pairs={{0,31},{1,0},{2,1},{3,2},{4,3},{5,4},{6,5},{7,6},{8,7},{9,8},{10,9... | collective-permute-start | bytes 49160 | tf_op jit(solution)/shard_map/ppermute | solution.py:16
  10.4 0.8 %collective-permute-start.2 = (bf16[8,8,128]{2,1,0:T(8,128)(2,1)}, bf16[8,8,128]{2,1,0:T(8,128)(2,1)S(1)}, u32[]{:S(2)}, u32[]{:S(2)}) collective-permute-start(bf16[8,8,128]{2,1,0:T(8,128)(2,1)} %get-tuple-element.16), channel_id=1, source_target_pairs={{0,1},{1,2},{2,3},{3,4},{4,5},{5,6},{6,7},{7,8},{8,9},{9,10},{10,1... | collective-permute-start | bytes 49160 | tf_op jit(solution)/shard_map/ppermute | solution.py:16
  11.2 0.0 collective-permute-start.3
  11.2 1.3 %copy.15.target_ref = s32[1,5,8]{2,1,0:T(8,128)} copy(s32[1,5,8]{2,0,1:T(1,128)} %param.14) | data formatting | bytes 320 | tf_op args[2]
  12.4 0.0 collective-permute-done.rest_0_
  12.4 0.0 copy-start.4
  12.4 0.3 collective-permute-done.1.rest_1_
  12.8 0.0 copy-start.5
  12.8 0.0 collective-permute-done.2.rest_3_
  12.8 0.0 copy-start.6
  12.8 4.8 %collective-permute-done.3.rest_4_ = bf16[8,8,128]{2,1,0:T(8,128)(2,1)S(1)} collective-permute-done((bf16[8,8,128]{2,1,0:T(8,128)(2,1)}, bf16[8,8,128]{2,1,0:T(8,128)(2,1)S(1)}, u32[]{:S(2)}, u32[]{:S(2)}) %collective-permute-start.3) | collective-permute-done | bytes 16416 | tf_op jit(solution)/shard_map/ppermute | solution.py:16
  17.6 0.0 copy-start.7
  17.6 0.0 copy-done.4
  17.6 0.0 copy-done.5
  17.6 0.0 copy-done.6
  17.6 0.6 %copy-done.7 = bf16[8,8,128]{2,1,0:T(8,128)(2,1)} copy-done((bf16[8,8,128]{2,1,0:T(8,128)(2,1)}, bf16[8,8,128]{2,1,0:T(8,128)(2,1)S(1)}, u32[]{:S(2)}) %copy-start.7) | copy-done | bytes 16408
  18.2 10.5 %mix.1 = (f32[8,4096]{1,0:T(8,128)}, f32[2,128,4096]{2,1,0:T(8,128)}, bf16[256,256]{1,0:T(8,128)(2,1)}, bf16[256,256]{1,0:T(8,128)(2,1)}, bf16[256,256]{1,0:T(8,128)(2,1)}, /*index=5*/bf16[256,256]{1,0:T(8,128)(2,1)}) custom-call(s32[1,5,8]{2,1,0:T(8,128)} %copy.15.target_ref, s32[1,5]{1,0:T(1,128)} %count_ref.1, f32[2,8]{1,0:T(2,128)} %coupling_ref.1, ...), custom_call_target="tpu_custom_call" | custom-call | tf_op jit(solution)/shard_map/mix/pallas_call | solution.py:185
  28.7 0.6 %collective-permute-start.4 = (bf16[256,256]{1,0:T(8,128)(2,1)}, bf16[256,256]{1,0:T(8,128)(2,1)S(1)}, u32[]{:S(2)}, u32[]{:S(2)}) collective-permute-start(bf16[256,256]{1,0:T(8,128)(2,1)} %get-tuple-element.19), channel_id=1, source_target_pairs={{0,30},{1,31},{2,0},{3,1},{4,2},{5,3},{6,4},{7,5},{8,6},{9,7},{10,... | collective-permute-start | bytes 393224 | tf_op jit(solution)/shard_map/ppermute | solution.py:16
  29.3 0.4 collective-permute-start.5
  29.7 1.6 %collective-permute-start.6 = (bf16[256,256]{1,0:T(8,128)(2,1)}, bf16[256,256]{1,0:T(8,128)(2,1)S(1)}, u32[]{:S(2)}, u32[]{:S(2)}) collective-permute-start(bf16[256,256]{1,0:T(8,128)(2,1)} %get-tuple-element.21), channel_id=1, source_target_pairs={{0,1},{1,2},{2,3},{3,4},{4,5},{5,6},{6,7},{7,8},{8,9},{9,10},{10,1... | collective-permute-start | bytes 393224 | tf_op jit(solution)/shard_map/ppermute | solution.py:16
  31.2 1.6 %collective-permute-start.7 = (bf16[256,256]{1,0:T(8,128)(2,1)}, bf16[256,256]{1,0:T(8,128)(2,1)S(1)}, u32[]{:S(2)}, u32[]{:S(2)}) collective-permute-start(bf16[256,256]{1,0:T(8,128)(2,1)} %get-tuple-element.22), channel_id=1, source_target_pairs={{0,2},{1,3},{2,4},{3,5},{4,6},{5,7},{6,8},{7,9},{8,10},{9,11},{10,... | collective-permute-start | bytes 393224 | tf_op jit(solution)/shard_map/ppermute | solution.py:16
  32.9 0.3 collective-permute-done.4.rest_0_
  33.1 0.0 copy-start
  33.1 4.3 %collective-permute-done.5.rest_1_ = bf16[256,256]{1,0:T(8,128)(2,1)S(1)} collective-permute-done((bf16[256,256]{1,0:T(8,128)(2,1)}, bf16[256,256]{1,0:T(8,128)(2,1)S(1)}, u32[]{:S(2)}, u32[]{:S(2)}) %collective-permute-start.5) | collective-permute-done | bytes 131104 | tf_op jit(solution)/shard_map/ppermute | solution.py:16
  37.4 0.0 copy-start.1
  37.4 0.0 collective-permute-done.6.rest_2_
  37.4 0.0 copy-start.2
  37.4 2.6 %collective-permute-done.7.rest_3_ = bf16[256,256]{1,0:T(8,128)(2,1)S(1)} collective-permute-done((bf16[256,256]{1,0:T(8,128)(2,1)}, bf16[256,256]{1,0:T(8,128)(2,1)S(1)}, u32[]{:S(2)}, u32[]{:S(2)}) %collective-permute-start.7) | collective-permute-done | bytes 131104 | tf_op jit(solution)/shard_map/ppermute | solution.py:16
  40.1 0.0 copy-start.3
  40.1 0.0 copy-done
  40.1 0.0 copy-done.1
  40.1 0.0 copy-done.2
  40.1 0.6 %copy-done.3 = bf16[256,256]{1,0:T(8,128)(2,1)} copy-done((bf16[256,256]{1,0:T(8,128)(2,1)}, bf16[256,256]{1,0:T(8,128)(2,1)S(1)}, u32[]{:S(2)}) %copy-start.3) | copy-done | bytes 131096
  40.7 9.1 %apply_halo.1 = f32[2,128,4096]{2,1,0:T(8,128)} custom-call(s32[1,4]{1,0:T(1,128)} %rows_ref.1, s32[8,128]{1,0:T(8,128)} %bitcast.8, s32[32,128]{1,0:T(8,128)} %bitcast.6, bf16[256,256]{1,0:T(8,128)(2,1)} %copy-done, bf16[256,256]{1,0:T(8,128)(2,1)} %copy-done.1, bf16[256,256]{1,0:T(8,128)(2,1)} %copy-done.2, bf16[256,256]{1,0:T(8,128)(2,1)} %copy-done.3, ...), custom_call_target="tpu_custom_call" | custom-call | tf_op jit(solution)/shard_map/apply_halo/pallas_call | solution.py:277
Async XLA Ops:
  3.4 9.1 %collective-permute-start = (bf16[8,8,128]{2,1,0:T(8,128)(2,1)}, bf16[8,8,128]{2,1,0:T(8,128)(2,1)S(1)}, u32[]{:S(2)}, u32[]{:S(2)}) collective-permute-start(bf16[8,8,128]{2,1,0:T(8,128)(2,1)} %get-tuple-element.13), channel_id=1, source_target_pairs={{0,30},{1,31},{2,0},{3,1},{4,2},{5,3},{6,4},{7,5},{8,6},{9,7},{10,... | collective-permute-start | bytes 49160 | tf_op jit(solution)/shard_map/ppermute | solution.py:16
  9.4 3.4 %collective-permute-start.1 = (bf16[8,8,128]{2,1,0:T(8,128)(2,1)}, bf16[8,8,128]{2,1,0:T(8,128)(2,1)S(1)}, u32[]{:S(2)}, u32[]{:S(2)}) collective-permute-start(bf16[8,8,128]{2,1,0:T(8,128)(2,1)} %get-tuple-element.14), channel_id=1, source_target_pairs={{0,31},{1,0},{2,1},{3,2},{4,3},{5,4},{6,5},{7,6},{8,7},{9,8},{10,9... | collective-permute-start | bytes 49160 | tf_op jit(solution)/shard_map/ppermute | solution.py:16
  10.4 2.4 %collective-permute-start.2 = (bf16[8,8,128]{2,1,0:T(8,128)(2,1)}, bf16[8,8,128]{2,1,0:T(8,128)(2,1)S(1)}, u32[]{:S(2)}, u32[]{:S(2)}) collective-permute-start(bf16[8,8,128]{2,1,0:T(8,128)(2,1)} %get-tuple-element.16), channel_id=1, source_target_pairs={{0,1},{1,2},{2,3},{3,4},{4,5},{5,6},{6,7},{7,8},{8,9},{9,10},{10,1... | collective-permute-start | bytes 49160 | tf_op jit(solution)/shard_map/ppermute | solution.py:16
  11.2 6.4 %collective-permute-start.3 = (bf16[8,8,128]{2,1,0:T(8,128)(2,1)}, bf16[8,8,128]{2,1,0:T(8,128)(2,1)S(1)}, u32[]{:S(2)}, u32[]{:S(2)}) collective-permute-start(bf16[8,8,128]{2,1,0:T(8,128)(2,1)} %get-tuple-element.17), channel_id=1, source_target_pairs={{0,2},{1,3},{2,4},{3,5},{4,6},{5,7},{6,8},{7,9},{8,10},{9,11},{10,... | collective-permute-start | bytes 49160 | tf_op jit(solution)/shard_map/ppermute | solution.py:16
  12.4 5.1 %copy-start.4 = (bf16[8,8,128]{2,1,0:T(8,128)(2,1)}, bf16[8,8,128]{2,1,0:T(8,128)(2,1)S(1)}, u32[]{:S(2)}) copy-start(bf16[8,8,128]{2,1,0:T(8,128)(2,1)S(1)} %collective-permute-done.rest_0_) | copy-start | bytes 49156
  12.8 4.8 %copy-start.5 = (bf16[8,8,128]{2,1,0:T(8,128)(2,1)}, bf16[8,8,128]{2,1,0:T(8,128)(2,1)S(1)}, u32[]{:S(2)}) copy-start(bf16[8,8,128]{2,1,0:T(8,128)(2,1)S(1)} %collective-permute-done.1.rest_1_) | copy-start | bytes 49156
  12.8 4.8 %copy-start.6 = (bf16[8,8,128]{2,1,0:T(8,128)(2,1)}, bf16[8,8,128]{2,1,0:T(8,128)(2,1)S(1)}, u32[]{:S(2)}) copy-start(bf16[8,8,128]{2,1,0:T(8,128)(2,1)S(1)} %collective-permute-done.2.rest_3_) | copy-start | bytes 49156
  17.6 0.6 %copy-start.7 = (bf16[8,8,128]{2,1,0:T(8,128)(2,1)}, bf16[8,8,128]{2,1,0:T(8,128)(2,1)S(1)}, u32[]{:S(2)}) copy-start(bf16[8,8,128]{2,1,0:T(8,128)(2,1)S(1)} %collective-permute-done.3.rest_4_) | copy-start | bytes 49156
  28.7 4.5 %collective-permute-start.4 = (bf16[256,256]{1,0:T(8,128)(2,1)}, bf16[256,256]{1,0:T(8,128)(2,1)S(1)}, u32[]{:S(2)}, u32[]{:S(2)}) collective-permute-start(bf16[256,256]{1,0:T(8,128)(2,1)} %get-tuple-element.19), channel_id=1, source_target_pairs={{0,30},{1,31},{2,0},{3,1},{4,2},{5,3},{6,4},{7,5},{8,6},{9,7},{10,... | collective-permute-start | bytes 393224 | tf_op jit(solution)/shard_map/ppermute | solution.py:16
  29.3 8.1 %collective-permute-start.5 = (bf16[256,256]{1,0:T(8,128)(2,1)}, bf16[256,256]{1,0:T(8,128)(2,1)S(1)}, u32[]{:S(2)}, u32[]{:S(2)}) collective-permute-start(bf16[256,256]{1,0:T(8,128)(2,1)} %get-tuple-element.20), channel_id=1, source_target_pairs={{0,31},{1,0},{2,1},{3,2},{4,3},{5,4},{6,5},{7,6},{8,7},{9,8},{10,9... | collective-permute-start | bytes 393224 | tf_op jit(solution)/shard_map/ppermute | solution.py:16
  29.7 7.8 %collective-permute-start.6 = (bf16[256,256]{1,0:T(8,128)(2,1)}, bf16[256,256]{1,0:T(8,128)(2,1)S(1)}, u32[]{:S(2)}, u32[]{:S(2)}) collective-permute-start(bf16[256,256]{1,0:T(8,128)(2,1)} %get-tuple-element.21), channel_id=1, source_target_pairs={{0,1},{1,2},{2,3},{3,4},{4,5},{5,6},{6,7},{7,8},{8,9},{9,10},{10,1... | collective-permute-start | bytes 393224 | tf_op jit(solution)/shard_map/ppermute | solution.py:16
  31.2 8.8 %collective-permute-start.7 = (bf16[256,256]{1,0:T(8,128)(2,1)}, bf16[256,256]{1,0:T(8,128)(2,1)S(1)}, u32[]{:S(2)}, u32[]{:S(2)}) collective-permute-start(bf16[256,256]{1,0:T(8,128)(2,1)} %get-tuple-element.22), channel_id=1, source_target_pairs={{0,2},{1,3},{2,4},{3,5},{4,6},{5,7},{6,8},{7,9},{8,10},{9,11},{10,... | collective-permute-start | bytes 393224 | tf_op jit(solution)/shard_map/ppermute | solution.py:16
  33.1 6.9 %copy-start = (bf16[256,256]{1,0:T(8,128)(2,1)}, bf16[256,256]{1,0:T(8,128)(2,1)S(1)}, u32[]{:S(2)}) copy-start(bf16[256,256]{1,0:T(8,128)(2,1)S(1)} %collective-permute-done.4.rest_0_) | copy-start | bytes 393220
  37.4 2.7 %copy-start.1 = (bf16[256,256]{1,0:T(8,128)(2,1)}, bf16[256,256]{1,0:T(8,128)(2,1)S(1)}, u32[]{:S(2)}) copy-start(bf16[256,256]{1,0:T(8,128)(2,1)S(1)} %collective-permute-done.5.rest_1_) | copy-start | bytes 393220
  37.4 2.6 %copy-start.2 = (bf16[256,256]{1,0:T(8,128)(2,1)}, bf16[256,256]{1,0:T(8,128)(2,1)S(1)}, u32[]{:S(2)}) copy-start(bf16[256,256]{1,0:T(8,128)(2,1)S(1)} %collective-permute-done.6.rest_2_) | copy-start | bytes 393220
  40.1 0.6 %copy-start.3 = (bf16[256,256]{1,0:T(8,128)(2,1)}, bf16[256,256]{1,0:T(8,128)(2,1)S(1)}, u32[]{:S(2)}) copy-start(bf16[256,256]{1,0:T(8,128)(2,1)S(1)} %collective-permute-done.7.rest_3_) | copy-start | bytes 393220

commit v2 on v1

v2 whole, which is shorter than its diff:
```python
import functools

import jax
import jax.numpy as jnp
from jax import lax
from jax.experimental import pallas as pl
from jax.experimental.pallas import tpu as pltpu
from jax.sharding import PartitionSpec as P

F32 = jnp.float32
BF16 = jnp.bfloat16


def shifted(array, axis, by):
    length = lax.axis_size(axis)
    return lax.ppermute(array, axis, [(i, (i + by) % length) for i in range(length)])


def vmem_out(shape, dtype):
    return pltpu.VMEM(shape, dtype)


def pinned(*arrays):
    return [pltpu.with_memory_space_constraint(a, pltpu.VMEM) for a in arrays]


def in_hbm(*arrays):
    return [pltpu.with_memory_space_constraint(a, pltpu.HBM) for a in arrays]


SMEM_SPEC = pl.BlockSpec(memory_space=pltpu.SMEM)
VMEM_SPEC = pl.BlockSpec(memory_space=pltpu.VMEM)
ANY_SPEC = pl.BlockSpec(memory_space=pl.ANY)
PARAMS = pltpu.CompilerParams(vmem_limit_bytes=16 * 2**20)


def select_kernel(send_ref, atm_ref, *out_refs):
    offsets, capacity = send_ref.shape[0], send_ref.shape[2]
    cells = out_refs[0].shape[-1]
    for d in range(offsets):
        for c in range(capacity):
            start = pl.multiple_of(send_ref[d, 0, c] * cells, cells)
            out_refs[d][c] = atm_ref[:, pl.ds(start, cells)]


def select_blocks(remap_send, atm_flux, cells):
    offsets, capacity = remap_send.shape[1], remap_send.shape[2]
    fluxes = atm_flux.shape[0]
    return pl.pallas_call(
        select_kernel,
        out_shape=[vmem_out((capacity, fluxes, cells), BF16)] * offsets,
        in_specs=[SMEM_SPEC, VMEM_SPEC],
        out_specs=[VMEM_SPEC] * offsets,
        compiler_params=PARAMS,
        name="select_blocks",
    )(*in_hbm(jnp.transpose(remap_send, (1, 0, 2)), atm_flux))


def split(x):
    high = x.astype(BF16)
    low = (x - high.astype(F32)).astype(BF16)
    return high, low


def lane_onehot(index_ref, cells):
    parts = []
    sub = lax.broadcasted_iota(jnp.int32, (cells, index_ref.shape[1]), 0)
    for q in range(index_ref.shape[0]):
        lane = index_ref[q : q + 1, :] & (cells - 1)
        parts.append(jnp.where(sub == lane, 1.0, 0.0).astype(BF16))
    return jnp.concatenate(parts, axis=1)


def block_mask(block_row, b):
    return jnp.where(block_row == b, 1.0, 0.0).astype(BF16)


def premix_kernel(
    wet_hbm, send_hbm, tracer_hbm, inverse_hbm, mixed, column, onehot, wetf,
    wet_ref, send_ref, base, tracer, inverse, small_sems, sems, *, group
):
    tracers, levels, ocean_cells = tracer.shape
    blocks, cells = wet_ref.shape
    small = (
        pltpu.make_async_copy(wet_hbm, wet_ref, small_sems.at[0]),
        pltpu.make_async_copy(send_hbm, send_ref, small_sems.at[1]),
    )
    for copy in small:
        copy.start()

    def load(g):
        lanes = pl.ds(g * group * cells, group * cells)
        rows = pl.ds(g * group, group)
        return (
            pltpu.make_async_copy(
                tracer_hbm.at[:, :, lanes], tracer.at[:, :, lanes], sems.at[0, g]
            ),
            pltpu.make_async_copy(inverse_hbm.at[rows], inverse.at[rows], sems.at[1, g]),
        )

    for g in range(blocks // group):
        for copy in load(g):
            copy.start()
    for copy in small:
        copy.wait()
    wetf[...] = wet_ref[...].astype(F32)
    base[...] = lane_onehot(send_ref, cells)
    block_row = jnp.concatenate(
        [send_ref[q : q + 1, :] // cells for q in range(send_ref.shape[0])], axis=1
    )
    for b in range(blocks):
        if b % group == 0:
            for copy in load(b // group):
                copy.wait()
        lanes = slice(b * cells, (b + 1) * cells)
        wet = wetf[b : b + 1, :]
        highs, lows, raw = [], [], []
        for t in range(tracers):
            value = tracer[t, :, lanes]
            raw.append(value)
            high, low = split(value)
            highs.append(high)
            lows.append(low)
        high = jnp.concatenate(highs, axis=1)
        low = jnp.concatenate(lows, axis=1)
        matrix = inverse[b]
        m_high, m_low = split(matrix)
        left = jnp.concatenate([m_high, m_low], axis=1)
        right = jnp.concatenate([high, high], axis=0)
        solved = jnp.dot(left, right, preferred_element_type=F32) + jnp.dot(
            m_high, low, preferred_element_type=F32
        )
        for t in range(tracers):
            mixed[t, :, lanes] = jnp.where(
                wet > 0.5, solved[:, t * cells : (t + 1) * cells], raw[t]
            )
        column[b] = jnp.broadcast_to(matrix[:, 0:1], (levels, cells))
        onehot[lanes, :] = base[...] * block_mask(block_row, b)


def premix(tracer, wet, mix_inverse, halo_send):
    tracers, levels, ocean_cells = tracer.shape
    blocks = mix_inverse.shape[0]
    cells = ocean_cells // blocks
    halo_count, depth, lanes = halo_send.shape[1:]
    picks = halo_count * depth * lanes
    group = 4 if blocks % 4 == 0 else 1
    return pl.pallas_call(
        functools.partial(premix_kernel, group=group),
        out_shape=[
            vmem_out(tracer.shape, F32),
            vmem_out((blocks, levels, cells), F32),
            vmem_out((ocean_cells, picks), BF16),
            vmem_out((blocks, cells), F32),
        ],
        in_specs=[ANY_SPEC] * 4,
        out_specs=[VMEM_SPEC] * 4,
        scratch_shapes=[
            pltpu.VMEM((blocks, cells), jnp.int32),
            pltpu.VMEM((halo_count * depth, lanes), jnp.int32),
            pltpu.VMEM((cells, picks), BF16),
            pltpu.VMEM(tracer.shape, F32),
            pltpu.VMEM(mix_inverse.shape, F32),
            pltpu.SemaphoreType.DMA((2,)),
            pltpu.SemaphoreType.DMA((2, blocks // group)),
        ],
        compiler_params=PARAMS,
        name="premix",
    )(
        *in_hbm(
            wet.reshape(blocks, cells),
            halo_send.reshape(halo_count * depth, lanes),
            tracer,
            mix_inverse,
        )
    )


def finish_kernel(target_ref, count_ref, coupling_ref, *rest, offsets, capacity):
    pieces = rest[:offsets]
    wet_ref, weights, mixed0, column, onehot = rest[offsets : offsets + 5]
    outs = rest[offsets + 5 :]
    flux_out, mixed = outs[:2]
    halo_count = offsets - 1
    halo_outs = outs[2 : 2 + halo_count]
    sent, acc = outs[2 + halo_count :]
    tracers, levels, ocean_cells = mixed0.shape
    blocks, cells = wet_ref.shape
    fluxes = flux_out.shape[0]

    acc[...] = jnp.zeros_like(acc)
    for d in range(offsets):
        for c in range(capacity):
            contrib = jnp.dot(
                pieces[d][c], weights[d * capacity + c], preferred_element_type=F32
            )
            used = jnp.where(c < count_ref[0, d], 1.0, 0.0).astype(F32)
            start = pl.multiple_of(target_ref[d, 0, c] * cells, cells)
            acc[:, pl.ds(start, cells)] += contrib * used

    sub = lax.broadcasted_iota(jnp.int32, (fluxes, cells), 0)
    couple = []
    for t in range(tracers):
        col = jnp.zeros((fluxes, cells), F32)
        for f in range(fluxes):
            col = jnp.where(sub == f, coupling_ref[t, f], col)
        couple.append(col)

    for b in range(blocks):
        lanes = slice(b * cells, (b + 1) * cells)
        flux = acc[:, lanes] * wet_ref[b : b + 1, :]
        flux_out[:, lanes] = flux
        for t in range(tracers):
            surface = jnp.sum(couple[t] * flux, axis=0, keepdims=True)
            value = mixed0[t, :, lanes] + column[b] * surface
            mixed[t, :, lanes] = value
            sent[t * levels : (t + 1) * levels, lanes] = value.astype(BF16)

    picks = onehot.shape[1] // halo_count
    for h in range(halo_count):
        halo_outs[h][...] = jnp.dot(
            sent[...], onehot[:, h * picks : (h + 1) * picks], preferred_element_type=F32
        ).astype(BF16)


def finish(pieces, remap_target, remap_counts, remap_weights, coupling, wetf, mixed0, column, onehot):
    offsets, capacity = remap_target.shape[1:]
    tracers, levels, ocean_cells = mixed0.shape
    cells = remap_weights.shape[-1]
    blocks = ocean_cells // cells
    fluxes = pieces[0].shape[1]
    halo_count = offsets - 1
    picks = onehot.shape[1] // halo_count
    return pl.pallas_call(
        functools.partial(finish_kernel, offsets=offsets, capacity=capacity),
        out_shape=[
            jax.ShapeDtypeStruct((fluxes, ocean_cells), F32),
            vmem_out(mixed0.shape, F32),
        ]
        + [vmem_out((tracers * levels, picks), BF16)] * halo_count,
        in_specs=[SMEM_SPEC] * 3 + [VMEM_SPEC] * (offsets + 5),
        out_specs=[VMEM_SPEC] * (2 + halo_count),
        scratch_shapes=[
            pltpu.VMEM((tracers * levels, ocean_cells), BF16),
            pltpu.VMEM((fluxes, ocean_cells), F32),
        ],
        input_output_aliases={3 + offsets + 2: 1},
        compiler_params=PARAMS,
        name="finish",
    )(
        jnp.transpose(remap_target, (1, 0, 2)),
        remap_counts,
        coupling,
        *pinned(*pieces, wetf),
        *pinned(remap_weights.reshape(offsets * capacity, cells, cells)),
        *pinned(mixed0, column, onehot),
    )


def preapply_kernel(rows_ref, ghost_ref, wet_ref, mixed, kept, onehot, base, *, halo_count, depth):
    tracers, levels, ocean_cells = mixed.shape
    blocks, cells = wet_ref.shape
    picks = onehot.shape[1]
    base[...] = lane_onehot(ghost_ref, cells)
    block_row = []
    for h in range(halo_count):
        for r in range(depth):
            q = h * depth + r
            block = ghost_ref[q : q + 1, :] // cells
            block_row.append(jnp.where(r < rows_ref[0, h], block, -1))
    block_row = jnp.concatenate(block_row, axis=1)
    ones = jnp.ones((16, picks), BF16)
    for b in range(blocks):
        lanes = slice(b * cells, (b + 1) * cells)
        hot = base[...] * block_mask(block_row, b)
        onehot[lanes, :] = hot
        count = lax.dot_general(
            ones, hot, (((1,), (1,)), ((), ())), preferred_element_type=F32
        )[0:1, :]
        keep = 1.0 - 0.25 * wet_ref[b : b + 1, :] * count
        for t in range(tracers):
            kept[t, :, lanes] = mixed[t, :, lanes] * keep


def preapply(mixed, wetf, halo_ghost, halo_rows):
    tracers, levels, ocean_cells = mixed.shape
    halo_count, depth, lanes = halo_ghost.shape[1:]
    cells = lanes
    blocks = ocean_cells // cells
    picks = halo_count * depth * lanes
    return pl.pallas_call(
        functools.partial(preapply_kernel, halo_count=halo_count, depth=depth),
        out_shape=[vmem_out(mixed.shape, F32), vmem_out((ocean_cells, picks), BF16)],
        in_specs=[SMEM_SPEC] + [VMEM_SPEC] * 3,
        out_specs=[VMEM_SPEC] * 2,
        scratch_shapes=[pltpu.VMEM((cells, picks), BF16)],
        input_output_aliases={3: 0},
        compiler_params=PARAMS,
        name="preapply",
    )(
        halo_rows,
        halo_ghost.reshape(halo_count * depth, lanes),
        *pinned(wetf, mixed),
    )


def apply_kernel(wet_ref, *rest, halo_count, group):
    values = rest[:halo_count]
    kept, onehot, out_hbm, staged, sems = rest[halo_count:]
    tracers, levels, ocean_cells = kept.shape
    blocks, cells = wet_ref.shape
    span = group * cells
    picks = values[0].shape[1]

    def store(g):
        lanes = pl.ds(g * span, span)
        return pltpu.make_async_copy(
            staged.at[:, :, lanes], out_hbm.at[:, :, lanes], sems.at[g]
        )

    left = jnp.concatenate([v[...] for v in values], axis=1)
    for g in range(blocks // group):
        total = lax.dot_general(
            left,
            onehot[g * span : (g + 1) * span, :],
            (((1,), (1,)), ((), ())),
            preferred_element_type=F32,
        )
        for i in range(group):
            b = g * group + i
            lanes = slice(b * cells, (b + 1) * cells)
            here = slice(i * cells, (i + 1) * cells)
            quarter = 0.25 * wet_ref[b : b + 1, :]
            for t in range(tracers):
                staged[t, :, lanes] = (
                    kept[t, :, lanes] + total[t * levels : (t + 1) * levels, here] * quarter
                )
        store(g).start()
    for g in range(blocks // group):
        store(g).wait()


def apply_halo(values, kept, onehot, wetf):
    tracers, levels, ocean_cells = kept.shape
    halo_count = len(values)
    picks = onehot.shape[1] // halo_count
    cells = wetf.shape[1]
    blocks = ocean_cells // cells
    group = 4 if blocks % 4 == 0 else 1
    return pl.pallas_call(
        functools.partial(apply_kernel, halo_count=halo_count, group=group),
        out_shape=jax.ShapeDtypeStruct(kept.shape, F32),
        in_specs=[VMEM_SPEC] * (halo_count + 3),
        out_specs=ANY_SPEC,
        scratch_shapes=[
            pltpu.VMEM(kept.shape, F32),
            pltpu.SemaphoreType.DMA((blocks // group,)),
        ],
        compiler_params=PARAMS,
        name="apply_halo",
    )(*pinned(wetf, *values, kept, onehot))


def body(
    atm_flux,
    remap_send,
    remap_target,
    remap_counts,
    remap_weights,
    coupling,
    tracer,
    wet,
    mix_inverse,
    halo_send,
    halo_ghost,
    halo_rows,
):
    offsets = remap_send.shape[1]
    radius = offsets // 2
    cells = remap_weights.shape[-1]
    outgoing = select_blocks(remap_send, atm_flux, cells)
    pieces = [
        outgoing[d] if d == radius else shifted(outgoing[d], "patch", d - radius)
        for d in range(offsets)
    ]
    mixed0, column, onehot, wetf = premix(tracer, wet, mix_inverse, halo_send)
    ocean_flux, mixed, *halo_out = finish(
        pieces, remap_target, remap_counts, remap_weights[0], coupling, wetf, mixed0, column, onehot
    )
    halo_offsets = [e for e in range(-radius, radius + 1) if e]
    values = [shifted(halo_out[h], "patch", halo_offsets[h]) for h in range(len(halo_out))]
    kept, ghosts = preapply(mixed, wetf, halo_ghost, halo_rows)
    return ocean_flux, apply_halo(values, kept, ghosts, wetf)


def solution(mesh):
    return jax.shard_map(
        body,
        mesh=mesh,
        in_specs=(
            P(None, "patch"),
            P("patch", None, None),
            P("patch", None, None),
            P("patch", None),
            P("patch", None, None, None, None),
            P(),
            P(None, None, "patch"),
            P("patch"),
            P("patch", None, None),
            P("patch", None, None, None),
            P("patch", None, None, None),
            P("patch", None),
        ),
        out_specs=(P(None, "patch"), P(None, None, "patch")),
        check_vma=False,
    )
```

time: 50.6 us -> 40.2 us (0.79); the launches traced: 49.9 us -> 40 us
  waiting for transfers between devices: 12.3 us -> 5.73 us
  local copies, waits for them, and re-layouts: 3.8 us -> 0.03 us
  starting transfers between devices: 11.9 us -> 14.5 us
  Pallas kernels: 21.1 us -> 19 us
    ppermute x8, waiting for transfers between devices: 12.3 us -> 5.73 us  [shifted(): lax.ppermute(array, axis, [(i, (i + by) % length) for i in range(length)])]
    unnamed x18 -> x12, local copies, waits for them, and re-layouts: 3.8 us -> 0.03 us
    ppermute x8, starting transfers between devices: 11.9 us -> 14.5 us  [shifted(): lax.ppermute(array, axis, [(i, (i + by) % length) for i in range(length)])]
    pallas_call x3 -> x5, Pallas kernels: 21.1 us -> 19 us  [the longest x1 5.98 us: premix(): pl.pallas_call(functools.partial(premix_kernel, group=group), out_shape=[...]
  transfers between devices with their start and end apart: 8 -> 8, of which waited for: 5 -> 2; matrix products, arithmetic and copies ran while one was open for 3% -> 0% of each run, Pallas kernels for 0% -> 24%
where the time goes in v2:
time: 40.2 us; the launch traced here: 40 us
  Pallas kernels  19 us (47%)
  starting transfers between devices  14.5 us (36%)
  waiting for transfers between devices  5.73 us (14%)
  between operations  0.77 us (2%)
    ppermute x8, starting transfers between devices, shifted(): lax.ppermute(array, axis, [(i, (i + by) % length) for i in range(length)])  14.5 us
    pallas_call x1, Pallas kernels, premix(): pl.pallas_call(functools.partial(premix_kernel, group=group), out_shape=[...  5.98 us
    ppermute x8, waiting for transfers between devices, shifted(): lax.ppermute(array, axis, [(i, (i + by) % length) for i in range(length)])  5.73 us
    pallas_call x1, Pallas kernels, finish(): pl.pallas_call(functools.partial(finish_kernel, offsets=offsets, capacity...  4.99 us
    pallas_call x1, Pallas kernels, preapply(): pl.pallas_call(functools.partial(preapply_kernel, halo_count=halo_count,...  3.71 us
    pallas_call x1, Pallas kernels, apply_halo(): pl.pallas_call(functools.partial(apply_kernel, halo_count=halo_count, gro...  3.34 us
    pallas_call x1, Pallas kernels, select_blocks(): pl.pallas_call(select_kernel, out_shape=[vmem_out((capacity, fluxes, cell...  0.96 us
  transfers between devices with their start and end apart: 8, of which 2 were waited for; matrix products, arithmetic and copies ran while one was open for 0% of the time, Pallas kernels for 24%

profile of v2, /device:TPU:1, one launch (start us, length us, event | category | flops | bytes accessed | tf_op | source)
XLA Modules:
  0.0 40.0 jit_solution(7241259877613706327)
XLA Ops:
  0.6 0.0 copy-start.3
  0.6 0.0 copy-start
  0.7 0.0 copy-start.4
  0.7 0.0 copy-start.2
  0.7 1.0 %select_blocks.1 = (bf16[8,8,128]{2,1,0:T(8,128)(2,1)S(1)}, bf16[8,8,128]{2,1,0:T(8,128)(2,1)S(1)}, bf16[8,8,128]{2,1,0:T(8,128)(2,1)S(1)}, bf16[8,8,128]{2,1,0:T(8,128)(2,1)S(1)}, bf16[8,8,128]{2,1,0:T(8,128)(2,1)S(1)}) custom-call(s32[5,1,8]{2,1,0:T(1,128)} %bitcast.11, bf16[8,3072]{1,0:T(8,128)(2,1)} %atm_ref.1), custom_call_target="tpu_custom_call" | custom-call | tf_op jit(solution)/shard_map/select_blocks/pallas_call | solution.py:49
  1.6 6.1 %collective-permute-start = (bf16[8,8,128]{2,1,0:T(8,128)(2,1)S(1)}, bf16[8,8,128]{2,1,0:T(8,128)(2,1)S(1)}, u32[]{:S(2)}, u32[]{:S(2)}) collective-permute-start(bf16[8,8,128]{2,1,0:T(8,128)(2,1)S(1)} %get-tuple-element.19), channel_id=1, source_target_pairs={{0,30},{1,31},{2,0},{3,1},{4,2},{5,3},{6,4},{7,5},{8,6},{9,7},{10,... | collective-permute-start | bytes 49160 | tf_op jit(solution)/shard_map/ppermute | solution.py:16
  7.7 1.0 %collective-permute-start.1 = (bf16[8,8,128]{2,1,0:T(8,128)(2,1)S(1)}, bf16[8,8,128]{2,1,0:T(8,128)(2,1)S(1)}, u32[]{:S(2)}, u32[]{:S(2)}) collective-permute-start(bf16[8,8,128]{2,1,0:T(8,128)(2,1)S(1)} %get-tuple-element.20), channel_id=1, source_target_pairs={{0,31},{1,0},{2,1},{3,2},{4,3},{5,4},{6,5},{7,6},{8,7},{9,8},{10,9... | collective-permute-start | bytes 49160 | tf_op jit(solution)/shard_map/ppermute | solution.py:16
  8.7 0.8 %collective-permute-start.2 = (bf16[8,8,128]{2,1,0:T(8,128)(2,1)S(1)}, bf16[8,8,128]{2,1,0:T(8,128)(2,1)S(1)}, u32[]{:S(2)}, u32[]{:S(2)}) collective-permute-start(bf16[8,8,128]{2,1,0:T(8,128)(2,1)S(1)} %get-tuple-element.22), channel_id=1, source_target_pairs={{0,1},{1,2},{2,3},{3,4},{4,5},{5,6},{6,7},{7,8},{8,9},{9,10},{10,1... | collective-permute-start | bytes 49160 | tf_op jit(solution)/shard_map/ppermute | solution.py:16
  9.5 0.0 collective-permute-start.3
  9.5 6.0 %premix.1 = (f32[2,128,4096]{2,1,0:T(8,128)S(1)}, f32[32,128,128]{2,1,0:T(8,128)S(1)}, bf16[4096,1024]{1,0:T(8,128)(2,1)S(1)}, f32[32,128]{1,0:T(8,128)S(1)}) custom-call(s32[32,128]{1,0:T(8,128)} %bitcast.9, s32[8,128]{1,0:T(8,128)} %bitcast.10, f32[2,128,4096]{2,1,0:T(8,128)} %tracer_hbm.1, f32[32,128,128]{2,1,0:T(8,128)} %inverse_hbm.1), custom_call_target="tpu_custom_call" | custom-call | tf_op jit(solution)/shard_map/premix/pallas_call | solution.py:148
  15.5 0.0 collective-permute-done.rest_0_
  15.5 0.0 collective-permute-done.1.rest_1_
  15.5 0.0 collective-permute-done.2.rest_3_
  15.5 0.2 collective-permute-done.3.rest_4_
  15.7 0.0 copy-done.3
  15.7 0.0 copy-done
  15.7 0.0 copy-done.4
  15.7 0.0 copy-done.2
  15.7 0.0 copy-start.1
  15.7 0.0 copy-start.5
  15.7 5.0 %finish.1 = (f32[8,4096]{1,0:T(8,128)}, f32[2,128,4096]{2,1,0:T(8,128)S(1)}, bf16[256,256]{1,0:T(8,128)(2,1)S(1)}, bf16[256,256]{1,0:T(8,128)(2,1)S(1)}, bf16[25...) custom-call(s32[5,1,8]{2,1,0:T(1,128)S(1)} %bitcast.8, ...), custom_call_target="tpu_custom_call", output_to_operand_aliasing={{1}: (10, {})} | custom-call | tf_op jit(solution)/shard_map/finish/pallas_call | solution.py:234
  20.7 4.9 %collective-permute-start.4 = (bf16[256,256]{1,0:T(8,128)(2,1)S(1)}, bf16[256,256]{1,0:T(8,128)(2,1)S(1)}, u32[]{:S(2)}, u32[]{:S(2)}) collective-permute-start(bf16[256,256]{1,0:T(8,128)(2,1)S(1)} %get-tuple-element.29), channel_id=1, source_target_pairs={{0,30},{1,31},{2,0},{3,1},{4,2},{5,3},{6,4},{7,5},{8,6},{9,7},{10,... | collective-permute-start | bytes 393224 | tf_op jit(solution)/shard_map/ppermute | solution.py:16
  25.6 0.3 collective-permute-start.5
  25.9 1.5 %collective-permute-start.6 = (bf16[256,256]{1,0:T(8,128)(2,1)S(1)}, bf16[256,256]{1,0:T(8,128)(2,1)S(1)}, u32[]{:S(2)}, u32[]{:S(2)}) collective-permute-start(bf16[256,256]{1,0:T(8,128)(2,1)S(1)} %get-tuple-element.31), channel_id=1, source_target_pairs={{0,1},{1,2},{2,3},{3,4},{4,5},{5,6},{6,7},{7,8},{8,9},{9,10},{10,1... | collective-permute-start | bytes 393224 | tf_op jit(solution)/shard_map/ppermute | solution.py:16
  27.4 0.0 collective-permute-start.7
  27.4 0.0 copy-done.1
  27.4 0.0 copy-done.5
  27.4 3.7 %preapply.1 = (f32[2,128,4096]{2,1,0:T(8,128)S(1)}, bf16[4096,1024]{1,0:T(8,128)(2,1)S(1)}) custom-call(s32[1,4]{1,0:T(1,128)S(1)} %copy-done.5, s32[8,128]{1,0:T(8,128)S(1)} %bitcast.7, f32[32,128]{1,0:T(8,128)S(1)} %get-tuple-element.24.rest_5_.wet_ref, f32[2,128,4096]{2,1,0:T(8,128)S(1)} %get-tuple-element.33.mixed), custom_call_target="tpu_custom_call", output_to_operand_aliasing={{0}: (3, {})} | custom-call | tf_op jit(solution)/shard_map/preapply/pallas_call | solution.py:291
  31.1 0.0 collective-permute-done.4.rest_0_
  31.1 0.0 collective-permute-done.5.rest_1_
  31.1 0.0 collective-permute-done.6.rest_2_
  31.1 5.6 %collective-permute-done.7.rest_3_ = bf16[256,256]{1,0:T(8,128)(2,1)S(1)} collective-permute-done((bf16[256,256]{1,0:T(8,128)(2,1)S(1)}, bf16[256,256]{1,0:T(8,128)(2,1)S(1)}, u32[]{:S(2)}, u32[]{:S(2)}) %collective-permute-start.7) | collective-permute-done | bytes 131104 | tf_op jit(solution)/shard_map/ppermute | solution.py:16
  36.7 3.3 %apply_halo.1 = f32[2,128,4096]{2,1,0:T(8,128)} custom-call(f32[32,128]{1,0:T(8,128)S(1)} %get-tuple-element.24.rest_5_.wet_ref, bf16[256,256]{1,0:T(8,128)(2,1)S(1)} %collective-permute-done.4.rest_0_, bf16[256,256]{1,0:T(8,128)(2,1)S(1)} %collective-permute-done.5.rest_1_, bf16[256,256]{1,0:T(8,128)(2,1)S(1)} %collective-permute-done.6.rest_2_, ...), custom_call_target="tpu_custom_call" | custom-call | tf_op jit(solution)/shard_map/apply_halo/pallas_call | solution.py:350
Async XLA Ops:
  0.6 15.0 %copy-start.3 = (f32[2,8]{1,0:T(2,128)S(1)}, f32[2,8]{1,0:T(2,128)}, u32[]{:S(2)}) copy-start(f32[2,8]{1,0:T(2,128)} %coupling_ref.1) | copy-start | bytes 196
  0.6 15.0 %copy-start = (bf16[1,5,8,128,128]{4,3,2,1,0:T(8,128)(2,1)S(1)}, bf16[1,5,8,128,128]{4,3,2,1,0:T(8,128)(2,1)}, u32[]{:S(2)}) copy-start(bf16[1,5,8,128,128]{4,3,2,1,0:T(8,128)(2,1)} %param.16) | copy-start | bytes 3932164
  0.7 15.0 %copy-start.4 = (s32[1,5]{1,0:T(1,128)S(1)}, s32[1,5]{1,0:T(1,128)}, u32[]{:S(2)}) copy-start(s32[1,5]{1,0:T(1,128)} %count_ref.1) | copy-start | bytes 64
  0.7 15.0 %copy-start.2 = (s32[1,5,8]{2,0,1:T(1,128)S(1)}, s32[1,5,8]{2,0,1:T(1,128)}, u32[]{:S(2)}) copy-start(s32[1,5,8]{2,0,1:T(1,128)} %param.14) | copy-start | bytes 484
  1.6 13.8 %collective-permute-start = (bf16[8,8,128]{2,1,0:T(8,128)(2,1)S(1)}, bf16[8,8,128]{2,1,0:T(8,128)(2,1)S(1)}, u32[]{:S(2)}, u32[]{:S(2)}) collective-permute-start(bf16[8,8,128]{2,1,0:T(8,128)(2,1)S(1)} %get-tuple-element.19), channel_id=1, source_target_pairs={{0,30},{1,31},{2,0},{3,1},{4,2},{5,3},{6,4},{7,5},{8,6},{9,7},{10,... | collective-permute-start | bytes 49160 | tf_op jit(solution)/shard_map/ppermute | solution.py:16
  7.7 7.8 %collective-permute-start.1 = (bf16[8,8,128]{2,1,0:T(8,128)(2,1)S(1)}, bf16[8,8,128]{2,1,0:T(8,128)(2,1)S(1)}, u32[]{:S(2)}, u32[]{:S(2)}) collective-permute-start(bf16[8,8,128]{2,1,0:T(8,128)(2,1)S(1)} %get-tuple-element.20), channel_id=1, source_target_pairs={{0,31},{1,0},{2,1},{3,2},{4,3},{5,4},{6,5},{7,6},{8,7},{9,8},{10,9... | collective-permute-start | bytes 49160 | tf_op jit(solution)/shard_map/ppermute | solution.py:16
  8.7 6.8 %collective-permute-start.2 = (bf16[8,8,128]{2,1,0:T(8,128)(2,1)S(1)}, bf16[8,8,128]{2,1,0:T(8,128)(2,1)S(1)}, u32[]{:S(2)}, u32[]{:S(2)}) collective-permute-start(bf16[8,8,128]{2,1,0:T(8,128)(2,1)S(1)} %get-tuple-element.22), channel_id=1, source_target_pairs={{0,1},{1,2},{2,3},{3,4},{4,5},{5,6},{6,7},{7,8},{8,9},{9,10},{10,1... | collective-permute-start | bytes 49160 | tf_op jit(solution)/shard_map/ppermute | solution.py:16
  9.5 6.2 %collective-permute-start.3 = (bf16[8,8,128]{2,1,0:T(8,128)(2,1)S(1)}, bf16[8,8,128]{2,1,0:T(8,128)(2,1)S(1)}, u32[]{:S(2)}, u32[]{:S(2)}) collective-permute-start(bf16[8,8,128]{2,1,0:T(8,128)(2,1)S(1)} %get-tuple-element.23), channel_id=1, source_target_pairs={{0,2},{1,3},{2,4},{3,5},{4,6},{5,7},{6,8},{7,9},{8,10},{9,11},{10,... | collective-permute-start | bytes 49160 | tf_op jit(solution)/shard_map/ppermute | solution.py:16
  15.7 11.7 %copy-start.1 = (s32[1,4,2,128]{3,2,1,0:T(2,128)S(1)}, s32[1,4,2,128]{3,2,1,0:T(2,128)}, u32[]{:S(2)}) copy-start(s32[1,4,2,128]{3,2,1,0:T(2,128)} %param.22) | copy-start | bytes 12292
  15.7 11.7 %copy-start.5 = (s32[1,4]{1,0:T(1,128)S(1)}, s32[1,4]{1,0:T(1,128)}, u32[]{:S(2)}) copy-start(s32[1,4]{1,0:T(1,128)} %rows_ref.1) | copy-start | bytes 52
  20.7 10.4 %collective-permute-start.4 = (bf16[256,256]{1,0:T(8,128)(2,1)S(1)}, bf16[256,256]{1,0:T(8,128)(2,1)S(1)}, u32[]{:S(2)}, u32[]{:S(2)}) collective-permute-start(bf16[256,256]{1,0:T(8,128)(2,1)S(1)} %get-tuple-element.29), channel_id=1, source_target_pairs={{0,30},{1,31},{2,0},{3,1},{4,2},{5,3},{6,4},{7,5},{8,6},{9,7},{10,... | collective-permute-start | bytes 393224 | tf_op jit(solution)/shard_map/ppermute | solution.py:16
  25.6 5.5 %collective-permute-start.5 = (bf16[256,256]{1,0:T(8,128)(2,1)S(1)}, bf16[256,256]{1,0:T(8,128)(2,1)S(1)}, u32[]{:S(2)}, u32[]{:S(2)}) collective-permute-start(bf16[256,256]{1,0:T(8,128)(2,1)S(1)} %get-tuple-element.30), channel_id=1, source_target_pairs={{0,31},{1,0},{2,1},{3,2},{4,3},{5,4},{6,5},{7,6},{8,7},{9,8},{10,9... | collective-permute-start | bytes 393224 | tf_op jit(solution)/shard_map/ppermute | solution.py:16
  25.9 5.2 %collective-permute-start.6 = (bf16[256,256]{1,0:T(8,128)(2,1)S(1)}, bf16[256,256]{1,0:T(8,128)(2,1)S(1)}, u32[]{:S(2)}, u32[]{:S(2)}) collective-permute-start(bf16[256,256]{1,0:T(8,128)(2,1)S(1)} %get-tuple-element.31), channel_id=1, source_target_pairs={{0,1},{1,2},{2,3},{3,4},{4,5},{5,6},{6,7},{7,8},{8,9},{9,10},{10,1... | collective-permute-start | bytes 393224 | tf_op jit(solution)/shard_map/ppermute | solution.py:16
  27.4 9.3 %collective-permute-start.7 = (bf16[256,256]{1,0:T(8,128)(2,1)S(1)}, bf16[256,256]{1,0:T(8,128)(2,1)S(1)}, u32[]{:S(2)}, u32[]{:S(2)}) collective-permute-start(bf16[256,256]{1,0:T(8,128)(2,1)S(1)} %get-tuple-element.32), channel_id=1, source_target_pairs={{0,2},{1,3},{2,4},{3,5},{4,6},{5,7},{6,8},{7,9},{8,10},{9,11},{10,... | collective-permute-start | bytes 393224 | tf_op jit(solution)/shard_map/ppermute | solution.py:16

commit v3 on v2

--- a/solution.py
+++ b/solution.py
@@ -14,6 +14,14 @@
 def shifted(array, axis, by):
     length = lax.axis_size(axis)
     return lax.ppermute(array, axis, [(i, (i + by) % length) for i in range(length)])
+
+
+def flux_order(radius):
+    return [e for e in range(-radius, radius + 1) if e]
+
+
+def halo_order(radius):
+    return list(range(radius, 0, -1)) + list(range(-radius, 0))
 
 
 def vmem_out(shape, dtype):
@@ -77,7 +85,7 @@
 
 def premix_kernel(
     wet_hbm, send_hbm, tracer_hbm, inverse_hbm, mixed, column, onehot, wetf,
-    wet_ref, send_ref, base, tracer, inverse, small_sems, sems, *, group
+    wet_ref, send_ref, base, tracer, inverse, small_sems, sems, *, cuts
 ):
     tracers, levels, ocean_cells = tracer.shape
     blocks, cells = wet_ref.shape
@@ -89,8 +97,9 @@
         copy.start()
 
     def load(g):
-        lanes = pl.ds(g * group * cells, group * cells)
-        rows = pl.ds(g * group, group)
+        first, size = cuts[g], cuts[g + 1] - cuts[g]
+        lanes = pl.ds(first * cells, size * cells)
+        rows = pl.ds(first, size)
         return (
             pltpu.make_async_copy(
                 tracer_hbm.at[:, :, lanes], tracer.at[:, :, lanes], sems.at[0, g]
@@ -98,7 +107,7 @@
             pltpu.make_async_copy(inverse_hbm.at[rows], inverse.at[rows], sems.at[1, g]),
         )
 
-    for g in range(blocks // group):
+    for g in range(len(cuts) - 1):
         for copy in load(g):
             copy.start()
     for copy in small:
@@ -109,8 +118,8 @@
         [send_ref[q : q + 1, :] // cells for q in range(send_ref.shape[0])], axis=1
     )
     for b in range(blocks):
-        if b % group == 0:
-            for copy in load(b // group):
+        if b in cuts:
+            for copy in load(cuts.index(b)):
                 copy.wait()
         lanes = slice(b * cells, (b + 1) * cells)
         wet = wetf[b : b + 1, :]
@@ -144,9 +153,9 @@
     cells = ocean_cells // blocks
     halo_count, depth, lanes = halo_send.shape[1:]
     picks = halo_count * depth * lanes
-    group = 4 if blocks % 4 == 0 else 1
+    cuts = (0, blocks // 4, blocks)
     return pl.pallas_call(
-        functools.partial(premix_kernel, group=group),
+        functools.partial(premix_kernel, cuts=cuts),
         out_shape=[
             vmem_out(tracer.shape, F32),
             vmem_out((blocks, levels, cells), F32),
@@ -162,7 +171,7 @@
             pltpu.VMEM(tracer.shape, F32),
             pltpu.VMEM(mix_inverse.shape, F32),
             pltpu.SemaphoreType.DMA((2,)),
-            pltpu.SemaphoreType.DMA((2, blocks // group)),
+            pltpu.SemaphoreType.DMA((2, len(cuts) - 1)),
         ],
         compiler_params=PARAMS,
         name="premix",
@@ -176,27 +185,40 @@
     )
 
 
-def finish_kernel(target_ref, count_ref, coupling_ref, *rest, offsets, capacity):
-    pieces = rest[:offsets]
+def finish_kernel(target_vmem, count_vmem, coupling_vmem, *rest, offsets, capacity):
+    radius = offsets // 2
+    order = flux_order(radius) + [0]
+    pieces = [rest[order.index(e)] for e in range(-radius, radius + 1)]
     wet_ref, weights, mixed0, column, onehot = rest[offsets : offsets + 5]
     outs = rest[offsets + 5 :]
     flux_out, mixed = outs[:2]
     halo_count = offsets - 1
     halo_outs = outs[2 : 2 + halo_count]
-    sent, acc = outs[2 + halo_count :]
+    sent, acc, parts, target_ref, count_ref, coupling_ref, sems = outs[2 + halo_count :]
     tracers, levels, ocean_cells = mixed0.shape
     blocks, cells = wet_ref.shape
     fluxes = flux_out.shape[0]
 
+    small = (
+        pltpu.make_async_copy(target_vmem, target_ref, sems.at[0]),
+        pltpu.make_async_copy(count_vmem, count_ref, sems.at[1]),
+        pltpu.make_async_copy(coupling_vmem, coupling_ref, sems.at[2]),
+    )
+    for copy in small:
+        copy.start()
     acc[...] = jnp.zeros_like(acc)
     for d in range(offsets):
         for c in range(capacity):
-            contrib = jnp.dot(
+            parts[d * capacity + c] = jnp.dot(
                 pieces[d][c], weights[d * capacity + c], preferred_element_type=F32
             )
+    for copy in small:
+        copy.wait()
+    for d in range(offsets):
+        for c in range(capacity):
             used = jnp.where(c < count_ref[0, d], 1.0, 0.0).astype(F32)
             start = pl.multiple_of(target_ref[d, 0, c] * cells, cells)
-            acc[:, pl.ds(start, cells)] += contrib * used
+            acc[:, pl.ds(start, cells)] += parts[d * capacity + c] * used
 
     sub = lax.broadcasted_iota(jnp.int32, (fluxes, cells), 0)
     couple = []
@@ -234,33 +256,36 @@
     return pl.pallas_call(
         functools.partial(finish_kernel, offsets=offsets, capacity=capacity),
         out_shape=[
-            jax.ShapeDtypeStruct((fluxes, ocean_cells), F32),
+            vmem_out((fluxes, ocean_cells), F32),
             vmem_out(mixed0.shape, F32),
         ]
         + [vmem_out((tracers * levels, picks), BF16)] * halo_count,
-        in_specs=[SMEM_SPEC] * 3 + [VMEM_SPEC] * (offsets + 5),
+        in_specs=[ANY_SPEC] * 3 + [VMEM_SPEC] * (offsets + 5),
         out_specs=[VMEM_SPEC] * (2 + halo_count),
         scratch_shapes=[
             pltpu.VMEM((tracers * levels, ocean_cells), BF16),
             pltpu.VMEM((fluxes, ocean_cells), F32),
+            pltpu.VMEM((offsets * capacity, fluxes, cells), F32),
+            pltpu.SMEM((offsets, 1, capacity), jnp.int32),
+            pltpu.SMEM(remap_counts.shape, jnp.int32),
+            pltpu.SMEM(coupling.shape, F32),
+            pltpu.SemaphoreType.DMA((3,)),
         ],
         input_output_aliases={3 + offsets + 2: 1},
         compiler_params=PARAMS,
         name="finish",
     )(
-        jnp.transpose(remap_target, (1, 0, 2)),
-        remap_counts,
-        coupling,
-        *pinned(*pieces, wetf),
+        *pinned(jnp.transpose(remap_target, (1, 0, 2)), remap_counts, coupling),
+        *pinned(*[pieces[e + offsets // 2] for e in flux_order(offsets // 2) + [0]], wetf),
         *pinned(remap_weights.reshape(offsets * capacity, cells, cells)),
         *pinned(mixed0, column, onehot),
     )
 
 
-def preapply_kernel(rows_ref, ghost_ref, wet_ref, mixed, kept, onehot, base, *, halo_count, depth):
-    tracers, levels, ocean_cells = mixed.shape
-    blocks, cells = wet_ref.shape
-    picks = onehot.shape[1]
+def ghost_kernel(
+    rows_ref, ghost_ref, wetf, mixed_unused, onehot, keep, base, *, halo_count, depth
+):
+    blocks, cells = wetf.shape
     base[...] = lane_onehot(ghost_ref, cells)
     block_row = []
     for h in range(halo_count):
@@ -269,45 +294,36 @@
             block = ghost_ref[q : q + 1, :] // cells
             block_row.append(jnp.where(r < rows_ref[0, h], block, -1))
     block_row = jnp.concatenate(block_row, axis=1)
-    ones = jnp.ones((16, picks), BF16)
     for b in range(blocks):
         lanes = slice(b * cells, (b + 1) * cells)
-        hot = base[...] * block_mask(block_row, b)
-        onehot[lanes, :] = hot
-        count = lax.dot_general(
-            ones, hot, (((1,), (1,)), ((), ())), preferred_element_type=F32
-        )[0:1, :]
-        keep = 1.0 - 0.25 * wet_ref[b : b + 1, :] * count
-        for t in range(tracers):
-            kept[t, :, lanes] = mixed[t, :, lanes] * keep
-
-
-def preapply(mixed, wetf, halo_ghost, halo_rows):
-    tracers, levels, ocean_cells = mixed.shape
+        onehot[lanes, :] = base[...] * block_mask(block_row, b)
+    ids = lax.broadcasted_iota(jnp.int32, (blocks, block_row.shape[1]), 0)
+    count = lax.dot_general(
+        block_mask(ids, block_row), base[...], (((1,), (1,)), ((), ())),
+        preferred_element_type=F32,
+    )
+    keep[...] = 1.0 - 0.25 * wetf[...] * count
+
+
+def ghost_onehot(halo_ghost, halo_rows, wetf, mixed):
     halo_count, depth, lanes = halo_ghost.shape[1:]
-    cells = lanes
-    blocks = ocean_cells // cells
     picks = halo_count * depth * lanes
     return pl.pallas_call(
-        functools.partial(preapply_kernel, halo_count=halo_count, depth=depth),
-        out_shape=[vmem_out(mixed.shape, F32), vmem_out((ocean_cells, picks), BF16)],
-        in_specs=[SMEM_SPEC] + [VMEM_SPEC] * 3,
+        functools.partial(ghost_kernel, halo_count=halo_count, depth=depth),
+        out_shape=[vmem_out((mixed.shape[2], picks), BF16), vmem_out(wetf.shape, F32)],
+        in_specs=[SMEM_SPEC, VMEM_SPEC, VMEM_SPEC, ANY_SPEC],
         out_specs=[VMEM_SPEC] * 2,
-        scratch_shapes=[pltpu.VMEM((cells, picks), BF16)],
-        input_output_aliases={3: 0},
+        scratch_shapes=[pltpu.VMEM((lanes, picks), BF16)],
         compiler_params=PARAMS,
-        name="preapply",
-    )(
-        halo_rows,
-        halo_ghost.reshape(halo_count * depth, lanes),
-        *pinned(wetf, mixed),
-    )
-
-
-def apply_kernel(wet_ref, *rest, halo_count, group):
-    values = rest[:halo_count]
-    kept, onehot, out_hbm, staged, sems = rest[halo_count:]
-    tracers, levels, ocean_cells = kept.shape
+        name="ghost_onehot",
+    )(halo_rows, halo_ghost.reshape(halo_count * depth, lanes), *pinned(wetf, mixed))
+
+
+def apply_kernel(wet_ref, keep_ref, *rest, halo_count, group):
+    radius = halo_count // 2
+    values = [rest[halo_order(radius).index(e)] for e in range(-radius, radius + 1) if e]
+    mixed, onehot, out_hbm, staged, sems = rest[halo_count:]
+    tracers, levels, ocean_cells = mixed.shape
     blocks, cells = wet_ref.shape
     span = group * cells
     picks = values[0].shape[1]
@@ -331,17 +347,19 @@
             lanes = slice(b * cells, (b + 1) * cells)
             here = slice(i * cells, (i + 1) * cells)
             quarter = 0.25 * wet_ref[b : b + 1, :]
+            keep = keep_ref[b : b + 1, :]
             for t in range(tracers):
                 staged[t, :, lanes] = (
-                    kept[t, :, lanes] + total[t * levels : (t + 1) * levels, here] * quarter
+                    mixed[t, :, lanes] * keep
+                    + total[t * levels : (t + 1) * levels, here] * quarter
                 )
         store(g).start()
     for g in range(blocks // group):
         store(g).wait()
 
 
-def apply_halo(values, kept, onehot, wetf):
-    tracers, levels, ocean_cells = kept.shape
+def apply_halo(values, mixed, onehot, wetf, keep):
+    tracers, levels, ocean_cells = mixed.shape
     halo_count = len(values)
     picks = onehot.shape[1] // halo_count
     cells = wetf.shape[1]
@@ -349,16 +367,16 @@
     group = 4 if blocks % 4 == 0 else 1
     return pl.pallas_call(
         functools.partial(apply_kernel, halo_count=halo_count, group=group),
-        out_shape=jax.ShapeDtypeStruct(kept.shape, F32),
-        in_specs=[VMEM_SPEC] * (halo_count + 3),
+        out_shape=jax.ShapeDtypeStruct(mixed.shape, F32),
+        in_specs=[VMEM_SPEC] * (halo_count + 4),
         out_specs=ANY_SPEC,
         scratch_shapes=[
-            pltpu.VMEM(kept.shape, F32),
+            pltpu.VMEM(mixed.shape, F32),
             pltpu.SemaphoreType.DMA((blocks // group,)),
         ],
         compiler_params=PARAMS,
         name="apply_halo",
-    )(*pinned(wetf, *values, kept, onehot))
+    )(*pinned(wetf, keep, *values, mixed, onehot))
 
 
 def body(
@@ -388,9 +406,13 @@
         pieces, remap_target, remap_counts, remap_weights[0], coupling, wetf, mixed0, column, onehot
     )
     halo_offsets = [e for e in range(-radius, radius + 1) if e]
-    values = [shifted(halo_out[h], "patch", halo_offsets[h]) for h in range(len(halo_out))]
-    kept, ghosts = preapply(mixed, wetf, halo_ghost, halo_rows)
-    return ocean_flux, apply_halo(values, kept, ghosts, wetf)
+    values = {}
+    for e in halo_order(radius):
+        values[e] = shifted(halo_out[halo_offsets.index(e)], "patch", e)
+    ghosts, keep = ghost_onehot(halo_ghost, halo_rows, wetf, mixed)
+    return ocean_flux, apply_halo(
+        [values[e] for e in halo_order(radius)], mixed, ghosts, wetf, keep
+    )
 
 
 def solution(mesh):

time: 40.2 us -> 34.2 us (0.85); the launches traced: 40 us -> 33.6 us
  Pallas kernels: 19 us -> 14.4 us
  waiting for transfers between devices: 5.73 us -> 3.43 us
  local copies, waits for them, and re-layouts: 0.03 us -> 0.68 us
    pallas_call x2, Pallas kernels: 9.69 us -> 6.08 us  [the longest x1 4.55 us: premix(): pl.pallas_call(functools.partial(premix_kernel, cuts=cuts), out_shape=[vm...]
    ppermute x8, waiting for transfers between devices: 5.73 us -> 3.43 us  [shifted(): lax.ppermute(array, axis, [(i, (i + by) % length) for i in range(length)])]
    pallas_call x1, Pallas kernels: 4.99 us -> 3.98 us  [finish(): pl.pallas_call(functools.partial(finish_kernel, offsets=offsets, capacity...]
    unnamed x12 -> x13, local copies, waits for them, and re-layouts: 0.03 us -> 0.68 us
  transfers between devices with their start and end apart: 8 -> 8, of which waited for: 2 -> 3; matrix products, arithmetic and copies ran while one was open for 0% -> 2% of each run, Pallas kernels for 24% -> 18%
where the time goes in v3:
time: 34.2 us; the launch traced here: 33.6 us
  Pallas kernels  14.4 us (42%)
  starting transfers between devices  14.3 us (42%)
  waiting for transfers between devices  3.43 us (10%)
  between operations  0.77 us (2%)
  local copies, waits for them, and re-layouts  0.68 us (2%)
    ppermute x8, starting transfers between devices, shifted(): lax.ppermute(array, axis, [(i, (i + by) % length) for i in range(length)])  14.3 us
    pallas_call x1, Pallas kernels, premix(): pl.pallas_call(functools.partial(premix_kernel, cuts=cuts), out_shape=[vm...  4.55 us
    pallas_call x1, Pallas kernels, finish(): pl.pallas_call(functools.partial(finish_kernel, offsets=offsets, capacity...  3.98 us
    ppermute x8, waiting for transfers between devices, shifted(): lax.ppermute(array, axis, [(i, (i + by) % length) for i in range(length)])  3.43 us
    pallas_call x1, Pallas kernels, apply_halo(): pl.pallas_call(functools.partial(apply_kernel, halo_count=halo_count, gro...  3.33 us
    pallas_call x1, Pallas kernels, ghost_onehot(): pl.pallas_call(functools.partial(ghost_kernel, halo_count=halo_count, dep...  1.53 us
    pallas_call x1, Pallas kernels, select_blocks(): pl.pallas_call(select_kernel, out_shape=[vmem_out((capacity, fluxes, cell...  0.96 us
    unnamed x13, local copies, waits for them, and re-layouts  0.68 us
  transfers between devices with their start and end apart: 8, of which 3 were waited for; matrix products, arithmetic and copies ran while one was open for 2% of the time, Pallas kernels for 18%

profile of v3, /device:TPU:1, one launch (start us, length us, event | category | flops | bytes accessed | tf_op | source)
XLA Modules:
  0.0 33.6 jit_solution(15035170075385614747)
XLA Ops:
  0.6 0.0 copy-start.3
  0.6 0.0 copy-start
  0.7 0.0 copy-start.4
  0.7 0.0 copy-start.2
  0.7 1.0 %select_blocks.1 = (bf16[8,8,128]{2,1,0:T(8,128)(2,1)S(1)}, bf16[8,8,128]{2,1,0:T(8,128)(2,1)S(1)}, bf16[8,8,128]{2,1,0:T(8,128)(2,1)S(1)}, bf16[8,8,128]{2,1,0:T(8,128)(2,1)S(1)}, bf16[8,8,128]{2,1,0:T(8,128)(2,1)S(1)}) custom-call(s32[5,1,8]{2,1,0:T(1,128)} %bitcast.11, bf16[8,3072]{1,0:T(8,128)(2,1)} %atm_ref.1), custom_call_target="tpu_custom_call" | custom-call | tf_op jit(solution)/shard_map/select_blocks/pallas_call | solution.py:57
  1.6 6.1 %collective-permute-start = (bf16[8,8,128]{2,1,0:T(8,128)(2,1)S(1)}, bf16[8,8,128]{2,1,0:T(8,128)(2,1)S(1)}, u32[]{:S(2)}, u32[]{:S(2)}) collective-permute-start(bf16[8,8,128]{2,1,0:T(8,128)(2,1)S(1)} %get-tuple-element.19), channel_id=1, source_target_pairs={{0,30},{1,31},{2,0},{3,1},{4,2},{5,3},{6,4},{7,5},{8,6},{9,7},{10,... | collective-permute-start | bytes 49160 | tf_op jit(solution)/shard_map/ppermute | solution.py:16
  7.7 1.0 %collective-permute-start.1 = (bf16[8,8,128]{2,1,0:T(8,128)(2,1)S(1)}, bf16[8,8,128]{2,1,0:T(8,128)(2,1)S(1)}, u32[]{:S(2)}, u32[]{:S(2)}) collective-permute-start(bf16[8,8,128]{2,1,0:T(8,128)(2,1)S(1)} %get-tuple-element.20), channel_id=1, source_target_pairs={{0,31},{1,0},{2,1},{3,2},{4,3},{5,4},{6,5},{7,6},{8,7},{9,8},{10,9... | collective-permute-start | bytes 49160 | tf_op jit(solution)/shard_map/ppermute | solution.py:16
  8.7 0.8 %collective-permute-start.2 = (bf16[8,8,128]{2,1,0:T(8,128)(2,1)S(1)}, bf16[8,8,128]{2,1,0:T(8,128)(2,1)S(1)}, u32[]{:S(2)}, u32[]{:S(2)}) collective-permute-start(bf16[8,8,128]{2,1,0:T(8,128)(2,1)S(1)} %get-tuple-element.21), channel_id=1, source_target_pairs={{0,1},{1,2},{2,3},{3,4},{4,5},{5,6},{6,7},{7,8},{8,9},{9,10},{10,1... | collective-permute-start | bytes 49160 | tf_op jit(solution)/shard_map/ppermute | solution.py:16
  9.5 0.0 collective-permute-start.3
  9.5 4.6 %premix.1 = (f32[2,128,4096]{2,1,0:T(8,128)S(1)}, f32[32,128,128]{2,1,0:T(8,128)S(1)}, bf16[4096,1024]{1,0:T(8,128)(2,1)S(1)}, f32[32,128]{1,0:T(8,128)S(1)}) custom-call(s32[32,128]{1,0:T(8,128)} %bitcast.9, s32[8,128]{1,0:T(8,128)} %bitcast.10, f32[2,128,4096]{2,1,0:T(8,128)} %tracer_hbm.1, f32[32,128,128]{2,1,0:T(8,128)} %inverse_hbm.1), custom_call_target="tpu_custom_call" | custom-call | tf_op jit(solution)/shard_map/premix/pallas_call | solution.py:157
  14.0 0.0 collective-permute-done.rest_0_
  14.0 0.0 collective-permute-done.1.rest_1_
  14.0 0.0 collective-permute-done.2.rest_2_
  14.1 1.6 %collective-permute-done.3.rest_3_ = bf16[8,8,128]{2,1,0:T(8,128)(2,1)S(1)} collective-permute-done((bf16[8,8,128]{2,1,0:T(8,128)(2,1)S(1)}, bf16[8,8,128]{2,1,0:T(8,128)(2,1)S(1)}, u32[]{:S(2)}, u32[]{:S(2)}) %collective-permute-start.3) | collective-permute-done | bytes 16416 | tf_op jit(solution)/shard_map/ppermute | solution.py:16
  15.7 0.0 copy-done.3
  15.7 0.0 copy-done
  15.7 0.0 copy-done.4
  15.7 0.0 copy-done.2
  15.7 0.0 copy-start.1
  15.7 0.0 copy-start.5
  15.7 4.0 %finish.1 = (f32[8,4096]{1,0:T(8,128)S(1)}, f32[2,128,4096]{2,1,0:T(8,128)S(1)}, bf16[256,256]{1,0:T(8,128)(2,1)S(1)}, bf16[256,256]{1,0:T(8,128)(2,1)S(1)}, bf1...) custom-call(s32[5,1,8]{2,1,0:T(1,128)S(1)} %bitcast.8, ...), custom_call_target="tpu_custom_call", output_to_operand_aliasing={{1}: (10, {})} | custom-call | tf_op jit(solution)/shard_map/finish/pallas_call | solution.py:256
  19.7 0.1 collective-permute-start.4
  19.7 0.1 collective-permute-start.5
  19.8 5.8 %collective-permute-start.6 = (bf16[256,256]{1,0:T(8,128)(2,1)S(1)}, bf16[256,256]{1,0:T(8,128)(2,1)S(1)}, u32[]{:S(2)}, u32[]{:S(2)}) collective-permute-start(bf16[256,256]{1,0:T(8,128)(2,1)S(1)} %get-tuple-element.33), channel_id=1, source_target_pairs={{0,30},{1,31},{2,0},{3,1},{4,2},{5,3},{6,4},{7,5},{8,6},{9,7},{10,... | collective-permute-start | bytes 393224 | tf_op jit(solution)/shard_map/ppermute | solution.py:16
  25.6 0.6 %collective-permute-start.7 = (bf16[256,256]{1,0:T(8,128)(2,1)S(1)}, bf16[256,256]{1,0:T(8,128)(2,1)S(1)}, u32[]{:S(2)}, u32[]{:S(2)}) collective-permute-start(bf16[256,256]{1,0:T(8,128)(2,1)S(1)} %get-tuple-element.34), channel_id=1, source_target_pairs={{0,31},{1,0},{2,1},{3,2},{4,3},{5,4},{6,5},{7,6},{8,7},{9,8},{10,9... | collective-permute-start | bytes 393224 | tf_op jit(solution)/shard_map/ppermute | solution.py:16
  26.2 0.7 %copy.16 = f32[8,4096]{1,0:T(8,128)} copy(f32[8,4096]{1,0:T(8,128)S(1)} %get-tuple-element.36) | data formatting | bytes 262144
  26.9 0.0 copy-done.1
  26.9 0.0 copy-done.5
  26.9 1.5 %ghost_onehot.1 = (bf16[4096,1024]{1,0:T(8,128)(2,1)S(1)}, f32[32,128]{1,0:T(8,128)S(1)}) custom-call(s32[1,4]{1,0:T(1,128)S(1)} %copy-done.5, s32[8,128]{1,0:T(8,128)S(1)} %bitcast.7, f32[32,128]{1,0:T(8,128)S(1)} %get-tuple-element.24.rest_5_.wetf.wet_ref, f32[2,128,4096]{2,1,0:T(8,128)S(1)} %get-tuple-element.29.mixed_unused.rest_4_), custom_call_target="tpu_custom_call" | custom-call | tf_op jit(solution)/shard_map/ghost_onehot/pallas_call | solution.py:311
  28.4 0.0 collective-permute-done.4.rest_0_
  28.4 0.2 collective-permute-done.5.rest_1_
  28.7 0.0 collective-permute-done.6.rest_2_
  28.7 1.6 %collective-permute-done.7.rest_3_ = bf16[256,256]{1,0:T(8,128)(2,1)S(1)} collective-permute-done((bf16[256,256]{1,0:T(8,128)(2,1)S(1)}, bf16[256,256]{1,0:T(8,128)(2,1)S(1)}, u32[]{:S(2)}, u32[]{:S(2)}) %collective-permute-start.7) | collective-permute-done | bytes 131104 | tf_op jit(solution)/shard_map/ppermute | solution.py:16
  30.3 3.3 %apply_halo.1 = f32[2,128,4096]{2,1,0:T(8,128)} custom-call(f32[32,128]{1,0:T(8,128)S(1)} %get-tuple-element.24.rest_5_.wetf.wet_ref, f32[32,128]{1,0:T(8,128)S(1)} %get-tuple-element.30.keep_ref, bf16[256,256]{1,0:T(8,128)(2,1)S(1)} %collective-permute-done.4.rest_0_, bf16[256,256]{1,0:T(8,128)(2,1)S(1)} %collective-permute-done.5.rest_1_, ...), custom_call_target="tpu_custom_call" | custom-call | tf_op jit(solution)/shard_map/apply_halo/pallas_call | solution.py:368
Async XLA Ops:
  0.6 15.0 %copy-start.3 = (f32[2,8]{1,0:T(2,128)S(1)}, f32[2,8]{1,0:T(2,128)}, u32[]{:S(2)}) copy-start(f32[2,8]{1,0:T(2,128)} %coupling_vmem.1) | copy-start | bytes 196
  0.6 15.0 %copy-start = (bf16[1,5,8,128,128]{4,3,2,1,0:T(8,128)(2,1)S(1)}, bf16[1,5,8,128,128]{4,3,2,1,0:T(8,128)(2,1)}, u32[]{:S(2)}) copy-start(bf16[1,5,8,128,128]{4,3,2,1,0:T(8,128)(2,1)} %param.16) | copy-start | bytes 3932164
  0.7 15.0 %copy-start.4 = (s32[1,5]{1,0:T(1,128)S(1)}, s32[1,5]{1,0:T(1,128)}, u32[]{:S(2)}) copy-start(s32[1,5]{1,0:T(1,128)} %count_vmem.1) | copy-start | bytes 64
  0.7 15.0 %copy-start.2 = (s32[1,5,8]{2,0,1:T(1,128)S(1)}, s32[1,5,8]{2,0,1:T(1,128)}, u32[]{:S(2)}) copy-start(s32[1,5,8]{2,0,1:T(1,128)} %param.14) | copy-start | bytes 484
  1.6 12.4 %collective-permute-start = (bf16[8,8,128]{2,1,0:T(8,128)(2,1)S(1)}, bf16[8,8,128]{2,1,0:T(8,128)(2,1)S(1)}, u32[]{:S(2)}, u32[]{:S(2)}) collective-permute-start(bf16[8,8,128]{2,1,0:T(8,128)(2,1)S(1)} %get-tuple-element.19), channel_id=1, source_target_pairs={{0,30},{1,31},{2,0},{3,1},{4,2},{5,3},{6,4},{7,5},{8,6},{9,7},{10,... | collective-permute-start | bytes 49160 | tf_op jit(solution)/shard_map/ppermute | solution.py:16
  7.7 6.3 %collective-permute-start.1 = (bf16[8,8,128]{2,1,0:T(8,128)(2,1)S(1)}, bf16[8,8,128]{2,1,0:T(8,128)(2,1)S(1)}, u32[]{:S(2)}, u32[]{:S(2)}) collective-permute-start(bf16[8,8,128]{2,1,0:T(8,128)(2,1)S(1)} %get-tuple-element.20), channel_id=1, source_target_pairs={{0,31},{1,0},{2,1},{3,2},{4,3},{5,4},{6,5},{7,6},{8,7},{9,8},{10,9... | collective-permute-start | bytes 49160 | tf_op jit(solution)/shard_map/ppermute | solution.py:16
  8.7 5.4 %collective-permute-start.2 = (bf16[8,8,128]{2,1,0:T(8,128)(2,1)S(1)}, bf16[8,8,128]{2,1,0:T(8,128)(2,1)S(1)}, u32[]{:S(2)}, u32[]{:S(2)}) collective-permute-start(bf16[8,8,128]{2,1,0:T(8,128)(2,1)S(1)} %get-tuple-element.21), channel_id=1, source_target_pairs={{0,1},{1,2},{2,3},{3,4},{4,5},{5,6},{6,7},{7,8},{8,9},{9,10},{10,1... | collective-permute-start | bytes 49160 | tf_op jit(solution)/shard_map/ppermute | solution.py:16
  9.5 6.2 %collective-permute-start.3 = (bf16[8,8,128]{2,1,0:T(8,128)(2,1)S(1)}, bf16[8,8,128]{2,1,0:T(8,128)(2,1)S(1)}, u32[]{:S(2)}, u32[]{:S(2)}) collective-permute-start(bf16[8,8,128]{2,1,0:T(8,128)(2,1)S(1)} %get-tuple-element.22), channel_id=1, source_target_pairs={{0,2},{1,3},{2,4},{3,5},{4,6},{5,7},{6,8},{7,9},{8,10},{9,11},{10,... | collective-permute-start | bytes 49160 | tf_op jit(solution)/shard_map/ppermute | solution.py:16
  15.7 11.2 %copy-start.1 = (s32[1,4,2,128]{3,2,1,0:T(2,128)S(1)}, s32[1,4,2,128]{3,2,1,0:T(2,128)}, u32[]{:S(2)}) copy-start(s32[1,4,2,128]{3,2,1,0:T(2,128)} %param.22) | copy-start | bytes 12292
  15.7 11.2 %copy-start.5 = (s32[1,4]{1,0:T(1,128)S(1)}, s32[1,4]{1,0:T(1,128)}, u32[]{:S(2)}) copy-start(s32[1,4]{1,0:T(1,128)} %rows_ref.1) | copy-start | bytes 52
  19.7 8.7 %collective-permute-start.4 = (bf16[256,256]{1,0:T(8,128)(2,1)S(1)}, bf16[256,256]{1,0:T(8,128)(2,1)S(1)}, u32[]{:S(2)}, u32[]{:S(2)}) collective-permute-start(bf16[256,256]{1,0:T(8,128)(2,1)S(1)} %get-tuple-element.31), channel_id=1, source_target_pairs={{0,2},{1,3},{2,4},{3,5},{4,6},{5,7},{6,8},{7,9},{8,10},{9,11},{10,... | collective-permute-start | bytes 393224 | tf_op jit(solution)/shard_map/ppermute | solution.py:16
  19.7 8.9 %collective-permute-start.5 = (bf16[256,256]{1,0:T(8,128)(2,1)S(1)}, bf16[256,256]{1,0:T(8,128)(2,1)S(1)}, u32[]{:S(2)}, u32[]{:S(2)}) collective-permute-start(bf16[256,256]{1,0:T(8,128)(2,1)S(1)} %get-tuple-element.32), channel_id=1, source_target_pairs={{0,1},{1,2},{2,3},{3,4},{4,5},{5,6},{6,7},{7,8},{8,9},{9,10},{10,1... | collective-permute-start | bytes 393224 | tf_op jit(solution)/shard_map/ppermute | solution.py:16
  19.8 8.9 %collective-permute-start.6 = (bf16[256,256]{1,0:T(8,128)(2,1)S(1)}, bf16[256,256]{1,0:T(8,128)(2,1)S(1)}, u32[]{:S(2)}, u32[]{:S(2)}) collective-permute-start(bf16[256,256]{1,0:T(8,128)(2,1)S(1)} %get-tuple-element.33), channel_id=1, source_target_pairs={{0,30},{1,31},{2,0},{3,1},{4,2},{5,3},{6,4},{7,5},{8,6},{9,7},{10,... | collective-permute-start | bytes 393224 | tf_op jit(solution)/shard_map/ppermute | solution.py:16
  25.6 4.6 %collective-permute-start.7 = (bf16[256,256]{1,0:T(8,128)(2,1)S(1)}, bf16[256,256]{1,0:T(8,128)(2,1)S(1)}, u32[]{:S(2)}, u32[]{:S(2)}) collective-permute-start(bf16[256,256]{1,0:T(8,128)(2,1)S(1)} %get-tuple-element.34), channel_id=1, source_target_pairs={{0,31},{1,0},{2,1},{3,2},{4,3},{5,4},{6,5},{7,6},{8,7},{9,8},{10,9... | collective-permute-start | bytes 393224 | tf_op jit(solution)/shard_map/ppermute | solution.py:16

commit v4 on v3

--- a/solution.py
+++ b/solution.py
@@ -16,11 +16,7 @@
     return lax.ppermute(array, axis, [(i, (i + by) % length) for i in range(length)])
 
 
-def flux_order(radius):
-    return [e for e in range(-radius, radius + 1) if e]
-
-
-def halo_order(radius):
+def start_order(radius):
     return list(range(radius, 0, -1)) + list(range(-radius, 0))
 
 
@@ -187,7 +183,7 @@
 
 def finish_kernel(target_vmem, count_vmem, coupling_vmem, *rest, offsets, capacity):
     radius = offsets // 2
-    order = flux_order(radius) + [0]
+    order = start_order(radius) + [0]
     pieces = [rest[order.index(e)] for e in range(-radius, radius + 1)]
     wet_ref, weights, mixed0, column, onehot = rest[offsets : offsets + 5]
     outs = rest[offsets + 5 :]
@@ -276,7 +272,7 @@
         name="finish",
     )(
         *pinned(jnp.transpose(remap_target, (1, 0, 2)), remap_counts, coupling),
-        *pinned(*[pieces[e + offsets // 2] for e in flux_order(offsets // 2) + [0]], wetf),
+        *pinned(*[pieces[e + offsets // 2] for e in start_order(offsets // 2) + [0]], wetf),
         *pinned(remap_weights.reshape(offsets * capacity, cells, cells)),
         *pinned(mixed0, column, onehot),
     )
@@ -321,7 +317,7 @@
 
 def apply_kernel(wet_ref, keep_ref, *rest, halo_count, group):
     radius = halo_count // 2
-    values = [rest[halo_order(radius).index(e)] for e in range(-radius, radius + 1) if e]
+    values = [rest[start_order(radius).index(e)] for e in range(-radius, radius + 1) if e]
     mixed, onehot, out_hbm, staged, sems = rest[halo_count:]
     tracers, levels, ocean_cells = mixed.shape
     blocks, cells = wet_ref.shape
@@ -407,11 +403,11 @@
     )
     halo_offsets = [e for e in range(-radius, radius + 1) if e]
     values = {}
-    for e in halo_order(radius):
+    for e in start_order(radius):
         values[e] = shifted(halo_out[halo_offsets.index(e)], "patch", e)
     ghosts, keep = ghost_onehot(halo_ghost, halo_rows, wetf, mixed)
     return ocean_flux, apply_halo(
-        [values[e] for e in halo_order(radius)], mixed, ghosts, wetf, keep
+        [values[e] for e in start_order(radius)], mixed, ghosts, wetf, keep
     )
 
 

time: 34.2 us -> 33.3 us (0.974); the launches traced: 33.6 us -> 33.1 us
  waiting for transfers between devices: 3.43 us -> 2.19 us
  starting transfers between devices: 14.3 us -> 15.1 us
    ppermute x8, waiting for transfers between devices: 3.43 us -> 2.19 us  [shifted(): lax.ppermute(array, axis, [(i, (i + by) % length) for i in range(length)])]
    ppermute x8, starting transfers between devices: 14.3 us -> 15.1 us  [shifted(): lax.ppermute(array, axis, [(i, (i + by) % length) for i in range(length)])]
  transfers between devices with their start and end apart: 8 -> 8, of which waited for: 3 -> 2; matrix products, arithmetic and copies ran while one was open for 2% -> 2% of each run, Pallas kernels for 18% -> 18%
where the time goes in v4:
time: 33.3 us; the launch traced here: 33.1 us
  starting transfers between devices  15.1 us (45%)
  Pallas kernels  14.3 us (43%)
  waiting for transfers between devices  2.19 us (7%)
  between operations  0.8 us (2%)
  local copies, waits for them, and re-layouts  0.68 us (2%)
    ppermute x8, starting transfers between devices, shifted(): lax.ppermute(array, axis, [(i, (i + by) % length) for i in range(length)])  15.1 us
    pallas_call x1, Pallas kernels, premix(): pl.pallas_call(functools.partial(premix_kernel, cuts=cuts), out_shape=[vm...  4.55 us
    pallas_call x1, Pallas kernels, finish(): pl.pallas_call(functools.partial(finish_kernel, offsets=offsets, capacity...  3.97 us
    pallas_call x1, Pallas kernels, apply_halo(): pl.pallas_call(functools.partial(apply_kernel, halo_count=halo_count, gro...  3.33 us
    ppermute x8, waiting for transfers between devices, shifted(): lax.ppermute(array, axis, [(i, (i + by) % length) for i in range(length)])  2.19 us
    pallas_call x1, Pallas kernels, ghost_onehot(): pl.pallas_call(functools.partial(ghost_kernel, halo_count=halo_count, dep...  1.53 us
    pallas_call x1, Pallas kernels, select_blocks(): pl.pallas_call(select_kernel, out_shape=[vmem_out((capacity, fluxes, cell...  0.96 us
    unnamed x13, local copies, waits for them, and re-layouts  0.68 us
  transfers between devices with their start and end apart: 8, of which 2 were waited for; matrix products, arithmetic and copies ran while one was open for 2% of the time, Pallas kernels for 18%

profile of v4, /device:TPU:1, one launch (start us, length us, event | category | flops | bytes accessed | tf_op | source)
XLA Modules:
  0.0 33.1 jit_solution(9465024785678091324)
XLA Ops:
  0.6 0.0 copy-start.3
  0.6 0.0 copy-start
  0.7 0.0 copy-start.4
  0.7 0.0 copy-start.2
  0.7 1.0 %select_blocks.1 = (bf16[8,8,128]{2,1,0:T(8,128)(2,1)S(1)}, bf16[8,8,128]{2,1,0:T(8,128)(2,1)S(1)}, bf16[8,8,128]{2,1,0:T(8,128)(2,1)S(1)}, bf16[8,8,128]{2,1,0:T(8,128)(2,1)S(1)}, bf16[8,8,128]{2,1,0:T(8,128)(2,1)S(1)}) custom-call(s32[5,1,8]{2,1,0:T(1,128)} %bitcast.11, bf16[8,3072]{1,0:T(8,128)(2,1)} %atm_ref.1), custom_call_target="tpu_custom_call" | custom-call | tf_op jit(solution)/shard_map/select_blocks/pallas_call | solution.py:53
  1.6 2.1 %collective-permute-start = (bf16[8,8,128]{2,1,0:T(8,128)(2,1)S(1)}, bf16[8,8,128]{2,1,0:T(8,128)(2,1)S(1)}, u32[]{:S(2)}, u32[]{:S(2)}) collective-permute-start(bf16[8,8,128]{2,1,0:T(8,128)(2,1)S(1)} %get-tuple-element.19), channel_id=1, source_target_pairs={{0,2},{1,3},{2,4},{3,5},{4,6},{5,7},{6,8},{7,9},{8,10},{9,11},{10,... | collective-permute-start | bytes 49160 | tf_op jit(solution)/shard_map/ppermute | solution.py:16
  3.7 2.1 %collective-permute-start.1 = (bf16[8,8,128]{2,1,0:T(8,128)(2,1)S(1)}, bf16[8,8,128]{2,1,0:T(8,128)(2,1)S(1)}, u32[]{:S(2)}, u32[]{:S(2)}) collective-permute-start(bf16[8,8,128]{2,1,0:T(8,128)(2,1)S(1)} %get-tuple-element.20), channel_id=1, source_target_pairs={{0,1},{1,2},{2,3},{3,4},{4,5},{5,6},{6,7},{7,8},{8,9},{9,10},{10,1... | collective-permute-start | bytes 49160 | tf_op jit(solution)/shard_map/ppermute | solution.py:16
  5.8 3.9 %collective-permute-start.2 = (bf16[8,8,128]{2,1,0:T(8,128)(2,1)S(1)}, bf16[8,8,128]{2,1,0:T(8,128)(2,1)S(1)}, u32[]{:S(2)}, u32[]{:S(2)}) collective-permute-start(bf16[8,8,128]{2,1,0:T(8,128)(2,1)S(1)} %get-tuple-element.21), channel_id=1, source_target_pairs={{0,30},{1,31},{2,0},{3,1},{4,2},{5,3},{6,4},{7,5},{8,6},{9,7},{10,... | collective-permute-start | bytes 49160 | tf_op jit(solution)/shard_map/ppermute | solution.py:16
  9.6 0.0 collective-permute-start.3
  9.6 4.5 %premix.1 = (f32[2,128,4096]{2,1,0:T(8,128)S(1)}, f32[32,128,128]{2,1,0:T(8,128)S(1)}, bf16[4096,1024]{1,0:T(8,128)(2,1)S(1)}, f32[32,128]{1,0:T(8,128)S(1)}) custom-call(s32[32,128]{1,0:T(8,128)} %bitcast.9, s32[8,128]{1,0:T(8,128)} %bitcast.10, f32[2,128,4096]{2,1,0:T(8,128)} %tracer_hbm.1, f32[32,128,128]{2,1,0:T(8,128)} %inverse_hbm.1), custom_call_target="tpu_custom_call" | custom-call | tf_op jit(solution)/shard_map/premix/pallas_call | solution.py:153
  14.2 0.0 collective-permute-done.rest_0_
  14.2 0.0 collective-permute-done.1.rest_1_
  14.2 0.0 collective-permute-done.2.rest_2_
  14.2 0.0 collective-permute-done.3.rest_3_
  14.2 0.0 copy-done.3
  14.2 0.0 copy-done
  14.3 0.0 copy-done.4
  14.3 0.0 copy-done.2
  14.3 0.0 copy-start.1
  14.3 0.0 copy-start.5
  14.3 4.0 %finish.1 = (f32[8,4096]{1,0:T(8,128)S(1)}, f32[2,128,4096]{2,1,0:T(8,128)S(1)}, bf16[256,256]{1,0:T(8,128)(2,1)S(1)}, bf16[256,256]{1,0:T(8,128)(2,1)S(1)}, bf1...) custom-call(s32[5,1,8]{2,1,0:T(1,128)S(1)} %bitcast.8, ...), custom_call_target="tpu_custom_call", output_to_operand_aliasing={{1}: (10, {})} | custom-call | tf_op jit(solution)/shard_map/finish/pallas_call | solution.py:252
  18.3 0.1 collective-permute-start.4
  18.3 1.8 %collective-permute-start.5 = (bf16[256,256]{1,0:T(8,128)(2,1)S(1)}, bf16[256,256]{1,0:T(8,128)(2,1)S(1)}, u32[]{:S(2)}, u32[]{:S(2)}) collective-permute-start(bf16[256,256]{1,0:T(8,128)(2,1)S(1)} %get-tuple-element.32), channel_id=1, source_target_pairs={{0,1},{1,2},{2,3},{3,4},{4,5},{5,6},{6,7},{7,8},{8,9},{9,10},{10,1... | collective-permute-start | bytes 393224 | tf_op jit(solution)/shard_map/ppermute | solution.py:16
  20.1 5.3 %collective-permute-start.6 = (bf16[256,256]{1,0:T(8,128)(2,1)S(1)}, bf16[256,256]{1,0:T(8,128)(2,1)S(1)}, u32[]{:S(2)}, u32[]{:S(2)}) collective-permute-start(bf16[256,256]{1,0:T(8,128)(2,1)S(1)} %get-tuple-element.33), channel_id=1, source_target_pairs={{0,30},{1,31},{2,0},{3,1},{4,2},{5,3},{6,4},{7,5},{8,6},{9,7},{10,... | collective-permute-start | bytes 393224 | tf_op jit(solution)/shard_map/ppermute | solution.py:16
  25.4 0.0 collective-permute-start.7
  25.4 0.7 %copy.16 = f32[8,4096]{1,0:T(8,128)} copy(f32[8,4096]{1,0:T(8,128)S(1)} %get-tuple-element.36) | data formatting | bytes 262144
  26.1 0.0 copy-done.1
  26.1 0.0 copy-done.5
  26.1 1.5 %ghost_onehot.1 = (bf16[4096,1024]{1,0:T(8,128)(2,1)S(1)}, f32[32,128]{1,0:T(8,128)S(1)}) custom-call(s32[1,4]{1,0:T(1,128)S(1)} %copy-done.5, s32[8,128]{1,0:T(8,128)S(1)} %bitcast.7, f32[32,128]{1,0:T(8,128)S(1)} %get-tuple-element.24.rest_5_.wetf.wet_ref, f32[2,128,4096]{2,1,0:T(8,128)S(1)} %get-tuple-element.29.mixed_unused.rest_4_), custom_call_target="tpu_custom_call" | custom-call | tf_op jit(solution)/shard_map/ghost_onehot/pallas_call | solution.py:307
  27.6 0.0 collective-permute-done.4.rest_0_
  27.6 0.0 collective-permute-done.5.rest_1_
  27.6 1.1 %collective-permute-done.6.rest_2_ = bf16[256,256]{1,0:T(8,128)(2,1)S(1)} collective-permute-done((bf16[256,256]{1,0:T(8,128)(2,1)S(1)}, bf16[256,256]{1,0:T(8,128)(2,1)S(1)}, u32[]{:S(2)}, u32[]{:S(2)}) %collective-permute-start.6) | collective-permute-done | bytes 131104 | tf_op jit(solution)/shard_map/ppermute | solution.py:16
  28.7 1.1 %collective-permute-done.7.rest_3_ = bf16[256,256]{1,0:T(8,128)(2,1)S(1)} collective-permute-done((bf16[256,256]{1,0:T(8,128)(2,1)S(1)}, bf16[256,256]{1,0:T(8,128)(2,1)S(1)}, u32[]{:S(2)}, u32[]{:S(2)}) %collective-permute-start.7) | collective-permute-done | bytes 131104 | tf_op jit(solution)/shard_map/ppermute | solution.py:16
  29.8 3.3 %apply_halo.1 = f32[2,128,4096]{2,1,0:T(8,128)} custom-call(f32[32,128]{1,0:T(8,128)S(1)} %get-tuple-element.24.rest_5_.wetf.wet_ref, f32[32,128]{1,0:T(8,128)S(1)} %get-tuple-element.30.keep_ref, bf16[256,256]{1,0:T(8,128)(2,1)S(1)} %collective-permute-done.4.rest_0_, bf16[256,256]{1,0:T(8,128)(2,1)S(1)} %collective-permute-done.5.rest_1_, ...), custom_call_target="tpu_custom_call" | custom-call | tf_op jit(solution)/shard_map/apply_halo/pallas_call | solution.py:364
Async XLA Ops:
  0.6 13.6 %copy-start.3 = (f32[2,8]{1,0:T(2,128)S(1)}, f32[2,8]{1,0:T(2,128)}, u32[]{:S(2)}) copy-start(f32[2,8]{1,0:T(2,128)} %coupling_vmem.1) | copy-start | bytes 196
  0.6 13.6 %copy-start = (bf16[1,5,8,128,128]{4,3,2,1,0:T(8,128)(2,1)S(1)}, bf16[1,5,8,128,128]{4,3,2,1,0:T(8,128)(2,1)}, u32[]{:S(2)}) copy-start(bf16[1,5,8,128,128]{4,3,2,1,0:T(8,128)(2,1)} %param.16) | copy-start | bytes 3932164
  0.7 13.6 %copy-start.4 = (s32[1,5]{1,0:T(1,128)S(1)}, s32[1,5]{1,0:T(1,128)}, u32[]{:S(2)}) copy-start(s32[1,5]{1,0:T(1,128)} %count_vmem.1) | copy-start | bytes 64
  0.7 13.6 %copy-start.2 = (s32[1,5,8]{2,0,1:T(1,128)S(1)}, s32[1,5,8]{2,0,1:T(1,128)}, u32[]{:S(2)}) copy-start(s32[1,5,8]{2,0,1:T(1,128)} %param.14) | copy-start | bytes 484
  1.6 12.5 %collective-permute-start = (bf16[8,8,128]{2,1,0:T(8,128)(2,1)S(1)}, bf16[8,8,128]{2,1,0:T(8,128)(2,1)S(1)}, u32[]{:S(2)}, u32[]{:S(2)}) collective-permute-start(bf16[8,8,128]{2,1,0:T(8,128)(2,1)S(1)} %get-tuple-element.19), channel_id=1, source_target_pairs={{0,2},{1,3},{2,4},{3,5},{4,6},{5,7},{6,8},{7,9},{8,10},{9,11},{10,... | collective-permute-start | bytes 49160 | tf_op jit(solution)/shard_map/ppermute | solution.py:16
  3.7 10.5 %collective-permute-start.1 = (bf16[8,8,128]{2,1,0:T(8,128)(2,1)S(1)}, bf16[8,8,128]{2,1,0:T(8,128)(2,1)S(1)}, u32[]{:S(2)}, u32[]{:S(2)}) collective-permute-start(bf16[8,8,128]{2,1,0:T(8,128)(2,1)S(1)} %get-tuple-element.20), channel_id=1, source_target_pairs={{0,1},{1,2},{2,3},{3,4},{4,5},{5,6},{6,7},{7,8},{8,9},{9,10},{10,1... | collective-permute-start | bytes 49160 | tf_op jit(solution)/shard_map/ppermute | solution.py:16
  5.8 8.4 %collective-permute-start.2 = (bf16[8,8,128]{2,1,0:T(8,128)(2,1)S(1)}, bf16[8,8,128]{2,1,0:T(8,128)(2,1)S(1)}, u32[]{:S(2)}, u32[]{:S(2)}) collective-permute-start(bf16[8,8,128]{2,1,0:T(8,128)(2,1)S(1)} %get-tuple-element.21), channel_id=1, source_target_pairs={{0,30},{1,31},{2,0},{3,1},{4,2},{5,3},{6,4},{7,5},{8,6},{9,7},{10,... | collective-permute-start | bytes 49160 | tf_op jit(solution)/shard_map/ppermute | solution.py:16
  9.6 4.6 %collective-permute-start.3 = (bf16[8,8,128]{2,1,0:T(8,128)(2,1)S(1)}, bf16[8,8,128]{2,1,0:T(8,128)(2,1)S(1)}, u32[]{:S(2)}, u32[]{:S(2)}) collective-permute-start(bf16[8,8,128]{2,1,0:T(8,128)(2,1)S(1)} %get-tuple-element.22), channel_id=1, source_target_pairs={{0,31},{1,0},{2,1},{3,2},{4,3},{5,4},{6,5},{7,6},{8,7},{9,8},{10,9... | collective-permute-start | bytes 49160 | tf_op jit(solution)/shard_map/ppermute | solution.py:16
  14.3 11.8 %copy-start.1 = (s32[1,4,2,128]{3,2,1,0:T(2,128)S(1)}, s32[1,4,2,128]{3,2,1,0:T(2,128)}, u32[]{:S(2)}) copy-start(s32[1,4,2,128]{3,2,1,0:T(2,128)} %param.22) | copy-start | bytes 12292
  14.3 11.8 %copy-start.5 = (s32[1,4]{1,0:T(1,128)S(1)}, s32[1,4]{1,0:T(1,128)}, u32[]{:S(2)}) copy-start(s32[1,4]{1,0:T(1,128)} %rows_ref.1) | copy-start | bytes 52
  18.3 9.3 %collective-permute-start.4 = (bf16[256,256]{1,0:T(8,128)(2,1)S(1)}, bf16[256,256]{1,0:T(8,128)(2,1)S(1)}, u32[]{:S(2)}, u32[]{:S(2)}) collective-permute-start(bf16[256,256]{1,0:T(8,128)(2,1)S(1)} %get-tuple-element.31), channel_id=1, source_target_pairs={{0,2},{1,3},{2,4},{3,5},{4,6},{5,7},{6,8},{7,9},{8,10},{9,11},{10,... | collective-permute-start | bytes 393224 | tf_op jit(solution)/shard_map/ppermute | solution.py:16
  18.3 9.3 %collective-permute-start.5 = (bf16[256,256]{1,0:T(8,128)(2,1)S(1)}, bf16[256,256]{1,0:T(8,128)(2,1)S(1)}, u32[]{:S(2)}, u32[]{:S(2)}) collective-permute-start(bf16[256,256]{1,0:T(8,128)(2,1)S(1)} %get-tuple-element.32), channel_id=1, source_target_pairs={{0,1},{1,2},{2,3},{3,4},{4,5},{5,6},{6,7},{7,8},{8,9},{9,10},{10,1... | collective-permute-start | bytes 393224 | tf_op jit(solution)/shard_map/ppermute | solution.py:16
  20.1 8.6 %collective-permute-start.6 = (bf16[256,256]{1,0:T(8,128)(2,1)S(1)}, bf16[256,256]{1,0:T(8,128)(2,1)S(1)}, u32[]{:S(2)}, u32[]{:S(2)}) collective-permute-start(bf16[256,256]{1,0:T(8,128)(2,1)S(1)} %get-tuple-element.33), channel_id=1, source_target_pairs={{0,30},{1,31},{2,0},{3,1},{4,2},{5,3},{6,4},{7,5},{8,6},{9,7},{10,... | collective-permute-start | bytes 393224 | tf_op jit(solution)/shard_map/ppermute | solution.py:16
  25.4 4.4 %collective-permute-start.7 = (bf16[256,256]{1,0:T(8,128)(2,1)S(1)}, bf16[256,256]{1,0:T(8,128)(2,1)S(1)}, u32[]{:S(2)}, u32[]{:S(2)}) collective-permute-start(bf16[256,256]{1,0:T(8,128)(2,1)S(1)} %get-tuple-element.34), channel_id=1, source_target_pairs={{0,31},{1,0},{2,1},{3,2},{4,3},{5,4},{6,5},{7,6},{8,7},{9,8},{10,9... | collective-permute-start | bytes 393224 | tf_op jit(solution)/shard_map/ppermute | solution.py:16

commit v5 on v4

--- a/solution.py
+++ b/solution.py
@@ -103,9 +103,8 @@
             pltpu.make_async_copy(inverse_hbm.at[rows], inverse.at[rows], sems.at[1, g]),
         )
 
-    for g in range(len(cuts) - 1):
-        for copy in load(g):
-            copy.start()
+    for copy in load(0):
+        copy.start()
     for copy in small:
         copy.wait()
     wetf[...] = wet_ref[...].astype(F32)
@@ -113,6 +112,12 @@
     block_row = jnp.concatenate(
         [send_ref[q : q + 1, :] // cells for q in range(send_ref.shape[0])], axis=1
     )
+    starts = {blocks // 4: 1, blocks * 3 // 4: 2}
+    for b in range(blocks):
+        if b in starts:
+            for copy in load(starts[b]):
+                copy.start()
+        onehot[b * cells : (b + 1) * cells, :] = base[...] * block_mask(block_row, b)
     for b in range(blocks):
         if b in cuts:
             for copy in load(cuts.index(b)):
@@ -140,7 +145,6 @@
                 wet > 0.5, solved[:, t * cells : (t + 1) * cells], raw[t]
             )
         column[b] = jnp.broadcast_to(matrix[:, 0:1], (levels, cells))
-        onehot[lanes, :] = base[...] * block_mask(block_row, b)
 
 
 def premix(tracer, wet, mix_inverse, halo_send):
@@ -149,7 +153,7 @@
     cells = ocean_cells // blocks
     halo_count, depth, lanes = halo_send.shape[1:]
     picks = halo_count * depth * lanes
-    cuts = (0, blocks // 4, blocks)
+    cuts = (0, blocks * 3 // 8, blocks * 3 // 4, blocks)
     return pl.pallas_call(
         functools.partial(premix_kernel, cuts=cuts),
         out_shape=[

time: 33.3 us -> 32.9 us (0.988)
  Pallas kernels: 14.3 us -> 13.9 us
    pallas_call x1, Pallas kernels: 4.55 us -> 4.05 us  [premix(): pl.pallas_call(functools.partial(premix_kernel, cuts=cuts), out_shape=[vm...]
  transfers between devices with their start and end apart: 8 -> 8, of which waited for: 2 -> 2; matrix products, arithmetic and copies ran while one was open for 2% -> 2% of each run, Pallas kernels for 18% -> 17%
where the time goes in v5:
time: 32.9 us; the launch traced here: 32.6 us
  starting transfers between devices  15.1 us (46%)
  Pallas kernels  13.9 us (42%)
  waiting for transfers between devices  2.19 us (7%)
  between operations  0.8 us (2%)
  local copies, waits for them, and re-layouts  0.68 us (2%)
    ppermute x8, starting transfers between devices, shifted(): lax.ppermute(array, axis, [(i, (i + by) % length) for i in range(length)])  15.1 us
    pallas_call x1, Pallas kernels, premix(): pl.pallas_call(functools.partial(premix_kernel, cuts=cuts), out_shape=[vm...  4.05 us
    pallas_call x1, Pallas kernels, finish(): pl.pallas_call(functools.partial(finish_kernel, offsets=offsets, capacity...  3.97 us
    pallas_call x1, Pallas kernels, apply_halo(): pl.pallas_call(functools.partial(apply_kernel, halo_count=halo_count, gro...  3.33 us
    ppermute x8, waiting for transfers between devices, shifted(): lax.ppermute(array, axis, [(i, (i + by) % length) for i in range(length)])  2.19 us
    pallas_call x1, Pallas kernels, ghost_onehot(): pl.pallas_call(functools.partial(ghost_kernel, halo_count=halo_count, dep...  1.53 us
    pallas_call x1, Pallas kernels, select_blocks(): pl.pallas_call(select_kernel, out_shape=[vmem_out((capacity, fluxes, cell...  0.96 us
    unnamed x13, local copies, waits for them, and re-layouts  0.68 us
  transfers between devices with their start and end apart: 8, of which 2 were waited for; matrix products, arithmetic and copies ran while one was open for 2% of the time, Pallas kernels for 17%

profile of v5, /device:TPU:1, one launch (start us, length us, event | category | flops | bytes accessed | tf_op | source)
XLA Modules:
  0.0 32.6 jit_solution(16852924674286626832)
XLA Ops:
  0.6 0.0 copy-start.3
  0.6 0.0 copy-start
  0.7 0.0 copy-start.4
  0.7 0.0 copy-start.2
  0.7 1.0 %select_blocks.1 = (bf16[8,8,128]{2,1,0:T(8,128)(2,1)S(1)}, bf16[8,8,128]{2,1,0:T(8,128)(2,1)S(1)}, bf16[8,8,128]{2,1,0:T(8,128)(2,1)S(1)}, bf16[8,8,128]{2,1,0:T(8,128)(2,1)S(1)}, bf16[8,8,128]{2,1,0:T(8,128)(2,1)S(1)}) custom-call(s32[5,1,8]{2,1,0:T(1,128)} %bitcast.11, bf16[8,3072]{1,0:T(8,128)(2,1)} %atm_ref.1), custom_call_target="tpu_custom_call" | custom-call | tf_op jit(solution)/shard_map/select_blocks/pallas_call | solution.py:53
  1.6 2.1 %collective-permute-start = (bf16[8,8,128]{2,1,0:T(8,128)(2,1)S(1)}, bf16[8,8,128]{2,1,0:T(8,128)(2,1)S(1)}, u32[]{:S(2)}, u32[]{:S(2)}) collective-permute-start(bf16[8,8,128]{2,1,0:T(8,128)(2,1)S(1)} %get-tuple-element.19), channel_id=1, source_target_pairs={{0,2},{1,3},{2,4},{3,5},{4,6},{5,7},{6,8},{7,9},{8,10},{9,11},{10,... | collective-permute-start | bytes 49160 | tf_op jit(solution)/shard_map/ppermute | solution.py:16
  3.7 2.1 %collective-permute-start.1 = (bf16[8,8,128]{2,1,0:T(8,128)(2,1)S(1)}, bf16[8,8,128]{2,1,0:T(8,128)(2,1)S(1)}, u32[]{:S(2)}, u32[]{:S(2)}) collective-permute-start(bf16[8,8,128]{2,1,0:T(8,128)(2,1)S(1)} %get-tuple-element.20), channel_id=1, source_target_pairs={{0,1},{1,2},{2,3},{3,4},{4,5},{5,6},{6,7},{7,8},{8,9},{9,10},{10,1... | collective-permute-start | bytes 49160 | tf_op jit(solution)/shard_map/ppermute | solution.py:16
  5.8 3.9 %collective-permute-start.2 = (bf16[8,8,128]{2,1,0:T(8,128)(2,1)S(1)}, bf16[8,8,128]{2,1,0:T(8,128)(2,1)S(1)}, u32[]{:S(2)}, u32[]{:S(2)}) collective-permute-start(bf16[8,8,128]{2,1,0:T(8,128)(2,1)S(1)} %get-tuple-element.21), channel_id=1, source_target_pairs={{0,30},{1,31},{2,0},{3,1},{4,2},{5,3},{6,4},{7,5},{8,6},{9,7},{10,... | collective-permute-start | bytes 49160 | tf_op jit(solution)/shard_map/ppermute | solution.py:16
  9.6 0.0 collective-permute-start.3
  9.6 4.1 %premix.1 = (f32[2,128,4096]{2,1,0:T(8,128)S(1)}, f32[32,128,128]{2,1,0:T(8,128)S(1)}, bf16[4096,1024]{1,0:T(8,128)(2,1)S(1)}, f32[32,128]{1,0:T(8,128)S(1)}) custom-call(s32[32,128]{1,0:T(8,128)} %bitcast.9, s32[8,128]{1,0:T(8,128)} %bitcast.10, f32[2,128,4096]{2,1,0:T(8,128)} %tracer_hbm.1, f32[32,128,128]{2,1,0:T(8,128)} %inverse_hbm.1), custom_call_target="tpu_custom_call" | custom-call | tf_op jit(solution)/shard_map/premix/pallas_call | solution.py:157
  13.7 0.0 collective-permute-done.rest_0_
  13.7 0.0 collective-permute-done.1.rest_1_
  13.7 0.0 collective-permute-done.2.rest_2_
  13.7 0.0 collective-permute-done.3.rest_3_
  13.7 0.0 copy-done.3
  13.7 0.0 copy-done
  13.8 0.0 copy-done.4
  13.8 0.0 copy-done.2
  13.8 0.0 copy-start.1
  13.8 0.0 copy-start.5
  13.8 4.0 %finish.1 = (f32[8,4096]{1,0:T(8,128)S(1)}, f32[2,128,4096]{2,1,0:T(8,128)S(1)}, bf16[256,256]{1,0:T(8,128)(2,1)S(1)}, bf16[256,256]{1,0:T(8,128)(2,1)S(1)}, bf1...) custom-call(s32[5,1,8]{2,1,0:T(1,128)S(1)} %bitcast.8, ...), custom_call_target="tpu_custom_call", output_to_operand_aliasing={{1}: (10, {})} | custom-call | tf_op jit(solution)/shard_map/finish/pallas_call | solution.py:256
  17.8 0.1 collective-permute-start.4
  17.8 1.8 %collective-permute-start.5 = (bf16[256,256]{1,0:T(8,128)(2,1)S(1)}, bf16[256,256]{1,0:T(8,128)(2,1)S(1)}, u32[]{:S(2)}, u32[]{:S(2)}) collective-permute-start(bf16[256,256]{1,0:T(8,128)(2,1)S(1)} %get-tuple-element.32), channel_id=1, source_target_pairs={{0,1},{1,2},{2,3},{3,4},{4,5},{5,6},{6,7},{7,8},{8,9},{9,10},{10,1... | collective-permute-start | bytes 393224 | tf_op jit(solution)/shard_map/ppermute | solution.py:16
  19.6 5.3 %collective-permute-start.6 = (bf16[256,256]{1,0:T(8,128)(2,1)S(1)}, bf16[256,256]{1,0:T(8,128)(2,1)S(1)}, u32[]{:S(2)}, u32[]{:S(2)}) collective-permute-start(bf16[256,256]{1,0:T(8,128)(2,1)S(1)} %get-tuple-element.33), channel_id=1, source_target_pairs={{0,30},{1,31},{2,0},{3,1},{4,2},{5,3},{6,4},{7,5},{8,6},{9,7},{10,... | collective-permute-start | bytes 393224 | tf_op jit(solution)/shard_map/ppermute | solution.py:16
  24.9 0.0 collective-permute-start.7
  24.9 0.7 %copy.16 = f32[8,4096]{1,0:T(8,128)} copy(f32[8,4096]{1,0:T(8,128)S(1)} %get-tuple-element.36) | data formatting | bytes 262144
  25.6 0.0 copy-done.1
  25.6 0.0 copy-done.5
  25.6 1.5 %ghost_onehot.1 = (bf16[4096,1024]{1,0:T(8,128)(2,1)S(1)}, f32[32,128]{1,0:T(8,128)S(1)}) custom-call(s32[1,4]{1,0:T(1,128)S(1)} %copy-done.5, s32[8,128]{1,0:T(8,128)S(1)} %bitcast.7, f32[32,128]{1,0:T(8,128)S(1)} %get-tuple-element.24.rest_5_.wetf.wet_ref, f32[2,128,4096]{2,1,0:T(8,128)S(1)} %get-tuple-element.29.mixed_unused.rest_4_), custom_call_target="tpu_custom_call" | custom-call | tf_op jit(solution)/shard_map/ghost_onehot/pallas_call | solution.py:311
  27.1 0.0 collective-permute-done.4.rest_0_
  27.1 0.0 collective-permute-done.5.rest_1_
  27.1 1.1 %collective-permute-done.6.rest_2_ = bf16[256,256]{1,0:T(8,128)(2,1)S(1)} collective-permute-done((bf16[256,256]{1,0:T(8,128)(2,1)S(1)}, bf16[256,256]{1,0:T(8,128)(2,1)S(1)}, u32[]{:S(2)}, u32[]{:S(2)}) %collective-permute-start.6) | collective-permute-done | bytes 131104 | tf_op jit(solution)/shard_map/ppermute | solution.py:16
  28.2 1.1 %collective-permute-done.7.rest_3_ = bf16[256,256]{1,0:T(8,128)(2,1)S(1)} collective-permute-done((bf16[256,256]{1,0:T(8,128)(2,1)S(1)}, bf16[256,256]{1,0:T(8,128)(2,1)S(1)}, u32[]{:S(2)}, u32[]{:S(2)}) %collective-permute-start.7) | collective-permute-done | bytes 131104 | tf_op jit(solution)/shard_map/ppermute | solution.py:16
  29.3 3.3 %apply_halo.1 = f32[2,128,4096]{2,1,0:T(8,128)} custom-call(f32[32,128]{1,0:T(8,128)S(1)} %get-tuple-element.24.rest_5_.wetf.wet_ref, f32[32,128]{1,0:T(8,128)S(1)} %get-tuple-element.30.keep_ref, bf16[256,256]{1,0:T(8,128)(2,1)S(1)} %collective-permute-done.4.rest_0_, bf16[256,256]{1,0:T(8,128)(2,1)S(1)} %collective-permute-done.5.rest_1_, ...), custom_call_target="tpu_custom_call" | custom-call | tf_op jit(solution)/shard_map/apply_halo/pallas_call | solution.py:368
Async XLA Ops:
  0.6 13.1 %copy-start.3 = (f32[2,8]{1,0:T(2,128)S(1)}, f32[2,8]{1,0:T(2,128)}, u32[]{:S(2)}) copy-start(f32[2,8]{1,0:T(2,128)} %coupling_vmem.1) | copy-start | bytes 196
  0.6 13.1 %copy-start = (bf16[1,5,8,128,128]{4,3,2,1,0:T(8,128)(2,1)S(1)}, bf16[1,5,8,128,128]{4,3,2,1,0:T(8,128)(2,1)}, u32[]{:S(2)}) copy-start(bf16[1,5,8,128,128]{4,3,2,1,0:T(8,128)(2,1)} %param.16) | copy-start | bytes 3932164
  0.7 13.1 %copy-start.4 = (s32[1,5]{1,0:T(1,128)S(1)}, s32[1,5]{1,0:T(1,128)}, u32[]{:S(2)}) copy-start(s32[1,5]{1,0:T(1,128)} %count_vmem.1) | copy-start | bytes 64
  0.7 13.1 %copy-start.2 = (s32[1,5,8]{2,0,1:T(1,128)S(1)}, s32[1,5,8]{2,0,1:T(1,128)}, u32[]{:S(2)}) copy-start(s32[1,5,8]{2,0,1:T(1,128)} %param.14) | copy-start | bytes 484
  1.6 12.1 %collective-permute-start = (bf16[8,8,128]{2,1,0:T(8,128)(2,1)S(1)}, bf16[8,8,128]{2,1,0:T(8,128)(2,1)S(1)}, u32[]{:S(2)}, u32[]{:S(2)}) collective-permute-start(bf16[8,8,128]{2,1,0:T(8,128)(2,1)S(1)} %get-tuple-element.19), channel_id=1, source_target_pairs={{0,2},{1,3},{2,4},{3,5},{4,6},{5,7},{6,8},{7,9},{8,10},{9,11},{10,... | collective-permute-start | bytes 49160 | tf_op jit(solution)/shard_map/ppermute | solution.py:16
  3.7 10.0 %collective-permute-start.1 = (bf16[8,8,128]{2,1,0:T(8,128)(2,1)S(1)}, bf16[8,8,128]{2,1,0:T(8,128)(2,1)S(1)}, u32[]{:S(2)}, u32[]{:S(2)}) collective-permute-start(bf16[8,8,128]{2,1,0:T(8,128)(2,1)S(1)} %get-tuple-element.20), channel_id=1, source_target_pairs={{0,1},{1,2},{2,3},{3,4},{4,5},{5,6},{6,7},{7,8},{8,9},{9,10},{10,1... | collective-permute-start | bytes 49160 | tf_op jit(solution)/shard_map/ppermute | solution.py:16
  5.8 7.9 %collective-permute-start.2 = (bf16[8,8,128]{2,1,0:T(8,128)(2,1)S(1)}, bf16[8,8,128]{2,1,0:T(8,128)(2,1)S(1)}, u32[]{:S(2)}, u32[]{:S(2)}) collective-permute-start(bf16[8,8,128]{2,1,0:T(8,128)(2,1)S(1)} %get-tuple-element.21), channel_id=1, source_target_pairs={{0,30},{1,31},{2,0},{3,1},{4,2},{5,3},{6,4},{7,5},{8,6},{9,7},{10,... | collective-permute-start | bytes 49160 | tf_op jit(solution)/shard_map/ppermute | solution.py:16
  9.6 4.1 %collective-permute-start.3 = (bf16[8,8,128]{2,1,0:T(8,128)(2,1)S(1)}, bf16[8,8,128]{2,1,0:T(8,128)(2,1)S(1)}, u32[]{:S(2)}, u32[]{:S(2)}) collective-permute-start(bf16[8,8,128]{2,1,0:T(8,128)(2,1)S(1)} %get-tuple-element.22), channel_id=1, source_target_pairs={{0,31},{1,0},{2,1},{3,2},{4,3},{5,4},{6,5},{7,6},{8,7},{9,8},{10,9... | collective-permute-start | bytes 49160 | tf_op jit(solution)/shard_map/ppermute | solution.py:16
  13.8 11.8 %copy-start.1 = (s32[1,4,2,128]{3,2,1,0:T(2,128)S(1)}, s32[1,4,2,128]{3,2,1,0:T(2,128)}, u32[]{:S(2)}) copy-start(s32[1,4,2,128]{3,2,1,0:T(2,128)} %param.22) | copy-start | bytes 12292
  13.8 11.8 %copy-start.5 = (s32[1,4]{1,0:T(1,128)S(1)}, s32[1,4]{1,0:T(1,128)}, u32[]{:S(2)}) copy-start(s32[1,4]{1,0:T(1,128)} %rows_ref.1) | copy-start | bytes 52
  17.8 9.3 %collective-permute-start.4 = (bf16[256,256]{1,0:T(8,128)(2,1)S(1)}, bf16[256,256]{1,0:T(8,128)(2,1)S(1)}, u32[]{:S(2)}, u32[]{:S(2)}) collective-permute-start(bf16[256,256]{1,0:T(8,128)(2,1)S(1)} %get-tuple-element.31), channel_id=1, source_target_pairs={{0,2},{1,3},{2,4},{3,5},{4,6},{5,7},{6,8},{7,9},{8,10},{9,11},{10,... | collective-permute-start | bytes 393224 | tf_op jit(solution)/shard_map/ppermute | solution.py:16
  17.8 9.3 %collective-permute-start.5 = (bf16[256,256]{1,0:T(8,128)(2,1)S(1)}, bf16[256,256]{1,0:T(8,128)(2,1)S(1)}, u32[]{:S(2)}, u32[]{:S(2)}) collective-permute-start(bf16[256,256]{1,0:T(8,128)(2,1)S(1)} %get-tuple-element.32), channel_id=1, source_target_pairs={{0,1},{1,2},{2,3},{3,4},{4,5},{5,6},{6,7},{7,8},{8,9},{9,10},{10,1... | collective-permute-start | bytes 393224 | tf_op jit(solution)/shard_map/ppermute | solution.py:16
  19.6 8.6 %collective-permute-start.6 = (bf16[256,256]{1,0:T(8,128)(2,1)S(1)}, bf16[256,256]{1,0:T(8,128)(2,1)S(1)}, u32[]{:S(2)}, u32[]{:S(2)}) collective-permute-start(bf16[256,256]{1,0:T(8,128)(2,1)S(1)} %get-tuple-element.33), channel_id=1, source_target_pairs={{0,30},{1,31},{2,0},{3,1},{4,2},{5,3},{6,4},{7,5},{8,6},{9,7},{10,... | collective-permute-start | bytes 393224 | tf_op jit(solution)/shard_map/ppermute | solution.py:16
  24.9 4.4 %collective-permute-start.7 = (bf16[256,256]{1,0:T(8,128)(2,1)S(1)}, bf16[256,256]{1,0:T(8,128)(2,1)S(1)}, u32[]{:S(2)}, u32[]{:S(2)}) collective-permute-start(bf16[256,256]{1,0:T(8,128)(2,1)S(1)} %get-tuple-element.34), channel_id=1, source_target_pairs={{0,31},{1,0},{2,1},{3,2},{4,3},{5,4},{6,5},{7,6},{8,7},{9,8},{10,9... | collective-permute-start | bytes 393224 | tf_op jit(solution)/shard_map/ppermute | solution.py:16
